TPU v7x, 32 devices: a 4x4x1 block of a 4x4x8 slice. The times are simulated.
32 devices in a mesh: batch: 1 (over z), g: 32 (over y, x, core).
Axes of the slice: x: 4, y: 4, z: 1, core: 2. Of those that a mesh axis runs over, the one named last changes fastest.
The devices are a block of a 4x4x8 slice.
Arguments:
- keys: float32 [65536], P(('batch', 'g'))
- payload: bfloat16 [65536, 1536], P(('batch', 'g'))
Outputs:
- output 1: float32 [131072], P(('batch', 'g'))
- output 2: bfloat16 [131072, 1536], P(('batch', 'g'))
- output 3: int32 [32], P(('batch', 'g'))
All inputs are finite; a program needn't handle non-finite values.
Results may differ from a plain program's by a relative error of at most 0.001.
Values are sent between devices in bfloat16 or wider.
A program may use at most 768 MiB of HBM per device.

v0:
```python
import jax
import jax.numpy as jnp
from jax import lax
from jax.sharding import PartitionSpec as P

PAD_KEY = 128.0


def solution(mesh):
    group_size = mesh.shape["g"]

    def local_part(keys_loc, rows_loc):
        n_dev = keys_loc.shape[0]
        width = rows_loc.shape[1]
        cap_rows = 2 * n_dev // group_size
        sorted_keys, sort_order = lax.sort((keys_loc, lax.iota(jnp.int32, n_dev)), num_keys=1)
        samples = sorted_keys[:: n_dev // group_size]
        all_samples = jnp.sort(lax.all_gather(samples, "g", tiled=True))
        splitters = all_samples[group_size + group_size // 2 :: group_size]
        edges = jnp.searchsorted(sorted_keys, splitters, side="left").astype(jnp.int32)
        starts = jnp.concatenate([jnp.zeros((1,), jnp.int32), edges])
        stops = jnp.concatenate([edges, jnp.full((1,), n_dev, jnp.int32)])
        src_pos = starts[:, None] + lax.iota(jnp.int32, cap_rows)[None, :]
        is_valid = src_pos < stops[:, None]
        src_pos = jnp.minimum(src_pos, n_dev - 1)
        send_keys = jnp.where(is_valid, sorted_keys[src_pos], PAD_KEY)
        send_rows = jnp.where(is_valid[:, :, None], rows_loc[sort_order[src_pos]], 0.0)
        recv_keys = lax.all_to_all(send_keys, "g", 0, 0, tiled=True)
        recv_rows = lax.all_to_all(send_rows, "g", 0, 0, tiled=True)
        flat_keys = recv_keys.reshape(-1)
        merged_keys, merge_order = lax.sort((flat_keys, lax.iota(jnp.int32, flat_keys.shape[0])), num_keys=1)
        merged_rows = recv_rows.reshape(-1, width)[merge_order]
        own_count = jnp.sum(flat_keys < PAD_KEY).astype(jnp.int32).reshape(1)
        return merged_keys, merged_rows, own_count

    row_spec = P(("batch", "g"))
    mat_spec = P(("batch", "g"), None)
    return jax.shard_map(local_part, mesh=mesh, in_specs=(row_spec, mat_spec), out_specs=(row_spec, mat_spec, row_spec), check_vma=False)
```

profile of v0, /device:TPU:103, one launch (start us, length us, event | category | flops | bytes accessed | tf_op | source)
XLA Modules:
  0.0 369.3 jit_solution(1947227641622224642)
XLA Ops:
  0.7 5.3 %sort.45 = (f32[2048]{0:T(1024)S(1)}, s32[2048]{0:T(1024)S(1)}) sort(f32[2048]{0:T(1024)} %param.4, s32[2048]{0:T(1024)S(1)} %iota.22), dimensions={0}, to_apply=%region_0.0 | sort | flops 22528 | bytes 32768 | tf_op jit(solution)/shard_map/sort | solution.py:16
  6.4 46.5 %all-reduce = f32[1024]{0:T(1024)S(1)} all-reduce(f32[1024]{0:T(1024)S(1)} %dynamic-update-slice), channel_id=1, replica_groups=mesh['batch'=1,'g'=32] {'g'}, use_global_device_ids=true, to_apply=%add | all-reduce | flops 1024 | bytes 8192
  52.9 4.5 %sort.46 = (f32[1024]{0:T(1024)S(1)}, s32[1024]{0:T(1024)}) sort(f32[1024]{0:T(1024)S(1)} %all-reduce, s32[1024]{0:T(1024)S(1)} %iota.23), dimensions={0}, to_apply=%region_1.0 | sort | flops 10240 | bytes 16384 | tf_op jit(solution)/shard_map/jit(sort)/sort | solution.py:18
  57.5 9.4 %while.24 = (s32[]{:T(128)}, u32[31]{0:T(128)S(1)}, u32[31]{0:T(128)S(1)}, f32[31]{0:T(128)S(1)}, pred[31]{0:T(512)(128)(4,1)S(1)}, /*index=5*/f32[2048]{0:T(1024)S(1)}, s32[]{:T(128)}, s32[]{:T(128)}, s32[]{}) while((s32[]{:T(128)}, u32[31]{0:T(128)S(1)}, u32[31]{0:T(128)S(1)}, f32[31]{0:T(128)S(1)}, pred[31]{0:T(512)(128)(4,1)S(1)}, ...), condition=%wide.region_3.4_spmd.clone, body=%wide.region_2.3_spmd.clone.sunk | while | flops 2051 | bytes 6414 | solution.py:20
  57.6 0.7 gather_fusion
  58.4 0.7 gather_fusion
  59.2 0.7 gather_fusion
  59.9 0.7 gather_fusion
  60.7 0.7 gather_fusion
  61.5 0.7 gather_fusion
  62.3 0.7 gather_fusion
  63.1 0.7 gather_fusion
  63.9 0.7 gather_fusion
  64.7 0.7 gather_fusion
  67.2 23.0 %gather_fusion.1 = f32[4096]{0:T(1024)S(1)} fusion(f32[2048]{0:T(1024)S(1)} %get-tuple-element.191, s32[4096]{0:T(1024)S(1)} %fusion.6), kind=kCustom, calls=%fused_computation.1 | custom fusion | bytes 49152 | tf_op jit(solution)/shard_map/gather | solution.py:26
  90.2 0.7 compare_select_fusion.5
  90.9 5.7 %all-to-all-start = ((f32[32,1,128]{2,1,0:T(1,128)}), f32[32,1,128]{2,1,0:T(1,128)S(1)}, u32[]{:S(2)}, u32[]{:S(2)}) async-start(f32[32,1,128]{2,1,0:T(1,128)} %compare_select_fusion.5), calls=%async_computation | async-start | bytes 32768 | tf_op jit(solution)/shard_map/all_to_all | solution.py:28
  96.8 23.0 %gather_fusion.2 = s32[4096]{0:T(1024)S(1)} fusion(s32[2048]{0:T(1024)S(1)} %get-tuple-element.84, s32[4096]{0:T(1024)S(1)} %fusion.6), kind=kCustom, calls=%fused_computation.2 | custom fusion | bytes 49152 | tf_op jit(solution)/shard_map/gather | solution.py:27
  119.8 28.8 %gather_fusion.3 = bf16[4096,1536]{1,0:T(8,128)(2,1)} fusion(bf16[2048,1536]{1,0:T(8,128)(2,1)} %param.5, s32[4096]{0:T(1024)S(1)} %fusion.8), kind=kCustom, calls=%fused_computation.3 | custom fusion | bytes 25182208 | tf_op jit(solution)/shard_map/gather | solution.py:27
  148.7 10.7 %broadcast_select_fusion.2 = bf16[32,128,1536]{2,1,0:T(8,128)(2,1)} fusion(bf16[32,128,1536]{2,1,0:T(8,128)(2,1)} %bitcast.15, pred[32,128]{1,0:T(8,128)(4,1)S(1)} %add_compare_fusion), kind=kLoop, calls=%fused_computation.19 | loop fusion | flops 6291456 | bytes 25169920 | tf_op jit(solution)/shard_map/jit(_where)/select_n | solution.py:27
  159.3 6.6 %all-to-all-start.1 = ((bf16[32,128,1536]{2,1,0:T(8,128)(2,1)}), bf16[32,128,1536]{2,1,0:T(8,128)(2,1)}, u32[]{:S(2)}, u32[]{:S(2)}) async-start(bf16[32,128,1536]{2,1,0:T(8,128)(2,1)} %broadcast_select_fusion.2), calls=%async_computation.1 | async-start | bytes 25165824 | tf_op jit(solution)/shard_map/all_to_all | solution.py:29
  165.9 6.0 %sort.47 = (f32[4096]{0:T(1024)}, s32[4096]{0:T(1024)S(1)}) sort(f32[4096]{0:T(1024)S(1)} %bitcast.16, s32[4096]{0:T(1024)S(1)} %iota.24), dimensions={0}, to_apply=%region_4.5 | sort | flops 49152 | bytes 65536 | tf_op jit(solution)/shard_map/sort | solution.py:31
  172.6 165.2 %all-to-all-done.1 = bf16[32,128,1536]{2,1,0:T(8,128)(2,1)} async-done(((bf16[32,128,1536]{2,1,0:T(8,128)(2,1)}), bf16[32,128,1536]{2,1,0:T(8,128)(2,1)}, u32[]{:S(2)}, u32[]{:S(2)}) %all-to-all-start.1) | async-done | bytes 12582944 | tf_op jit(solution)/shard_map/all_to_all | solution.py:29
  337.8 31.4 %gather_fusion.4 = bf16[4096,1536]{1,0:T(8,128)(2,1)} fusion(bf16[4096,1536]{1,0:T(8,128)(2,1)} %bitcast.6, s32[4096]{0:T(1024)S(1)} %fusion.9), kind=kCustom, calls=%fused_computation.4 | custom fusion | bytes 25182208 | tf_op jit(solution)/shard_map/gather | solution.py:32
  (81 shorter events, 3.3 us)
Async XLA Ops:
  90.9 68.4 %all-to-all-start = ((f32[32,1,128]{2,1,0:T(1,128)}), f32[32,1,128]{2,1,0:T(1,128)S(1)}, u32[]{:S(2)}, u32[]{:S(2)}) async-start(f32[32,1,128]{2,1,0:T(1,128)} %compare_select_fusion.5), calls=%async_computation | async-start | bytes 32768 | tf_op jit(solution)/shard_map/all_to_all | solution.py:28
  159.3 178.5 %all-to-all-start.1 = ((bf16[32,128,1536]{2,1,0:T(8,128)(2,1)}), bf16[32,128,1536]{2,1,0:T(8,128)(2,1)}, u32[]{:S(2)}, u32[]{:S(2)}) async-start(bf16[32,128,1536]{2,1,0:T(8,128)(2,1)} %broadcast_select_fusion.2), calls=%async_computation.1 | async-start | bytes 25165824 | tf_op jit(solution)/shard_map/all_to_all | solution.py:29
where the time goes:
time: 370 us; the launch traced here: 369 us
  waiting for transfers between devices  165 us (45%)
  local copies, waits for them, and re-layouts  115 us (31%)
  blocking collectives  46.5 us (13%)
  other arithmetic  28.7 us (8%)
  starting transfers between devices  12.3 us (3%)
    all_to_all x1, waiting for transfers between devices, local_part(): recv_rows = lax.all_to_all(send_rows, 'g', 0, 0, tiled=True)  165 us
    unnamed x1, blocking collectives  46.5 us
    gather x1, local copies, waits for them, and re-layouts, local_part(): merged_rows = recv_rows.reshape(-1, width)[merge_order]  31.4 us
    gather x1, local copies, waits for them, and re-layouts, local_part(): rows_loc[sort_order[src_pos]]  28.8 us
    gather x1, local copies, waits for them, and re-layouts, local_part(): send_keys = jnp.where(is_valid, sorted_keys[src_pos], PAD_KEY)  23 us
    gather x1, local copies, waits for them, and re-layouts, local_part(): sort_order[src_pos]  23 us
    select_n x1, other arithmetic, local_part(): jnp.where(is_valid[:, :, None], rows_loc[sort_order[src_pos]], 0.0)  10.7 us
    gather x12, local copies, waits for them, and re-layouts, local_part(): jnp.searchsorted(sorted_keys, splitters, side='left').astype(jnp.int32)  8.41 us
  transfers between devices with their start and end apart: 2, of which 1 were waited for; matrix products, arithmetic and copies ran while one was open for 19% of the time, Pallas kernels for 0%

commit v1 on v0

v1 whole, which is shorter than its diff:
```python
import functools

import jax
import jax.numpy as jnp
from jax import lax
from jax.experimental import pallas as pl
from jax.experimental.pallas import tpu as pltpu
from jax.sharding import PartitionSpec as P

PAD_KEY = 128.0
LANES = 128
SUB = 4
BASE = 65
RELAY = 2

VMEM = pl.BlockSpec(memory_space=pltpu.VMEM)
SMEM = pl.BlockSpec(memory_space=pltpu.SMEM)
ANY = pl.BlockSpec(memory_space=pl.ANY)


def share_keys_kernel(group_size, keys_ref, all_ref, send_sem, recv_sem):
    me = lax.axis_index("g")
    barrier = pltpu.get_barrier_semaphore()
    for d in range(1, group_size):
        pl.semaphore_signal(barrier, inc=1, device_id={"g": lax.rem(me + d, group_size)}, device_id_type=pl.DeviceIdType.MESH)
    pl.semaphore_wait(barrier, group_size - 1)
    copies = []
    for d in range(1, group_size):
        copies.append(
            pltpu.make_async_remote_copy(
                src_ref=keys_ref,
                dst_ref=all_ref.at[me],
                send_sem=send_sem.at[d],
                recv_sem=recv_sem.at[d],
                device_id={"g": lax.rem(me + d, group_size)},
                device_id_type=pl.DeviceIdType.MESH,
            )
        )
        copies[-1].start()
    all_ref[pl.ds(me, 1)] = keys_ref[...][None]
    for c in copies:
        c.wait()


def share_keys(keys, group_size):
    return pl.pallas_call(
        functools.partial(share_keys_kernel, group_size),
        out_shape=jax.ShapeDtypeStruct((group_size, *keys.shape), keys.dtype),
        in_specs=[VMEM],
        out_specs=VMEM,
        scratch_shapes=[pltpu.SemaphoreType.DMA((group_size,)), pltpu.SemaphoreType.DMA((group_size,))],
        compiler_params=pltpu.CompilerParams(collective_id=0, has_side_effects=True),
        name="share_keys",
    )(keys)


def split_rows_kernel(rows_ref, out_ref):
    tiles = rows_ref.shape[1] // LANES
    parts = tiles // SUB

    def body(g, carry):
        r = pl.multiple_of(g * 16, 16)
        v = rows_ref[pl.ds(r, 16), :].reshape(16, tiles, LANES)
        for q in range(parts):
            out_ref[pl.ds(r, 16), q] = v[:, SUB * q : SUB * (q + 1)]
        return carry

    lax.fori_loop(0, rows_ref.shape[0] // 16, body, 0)


def split_rows(rows):
    n, width = rows.shape
    block = 256
    shape = (n, width // (SUB * LANES), SUB, LANES)
    return pl.pallas_call(
        split_rows_kernel,
        grid=(n // block,),
        out_shape=jax.ShapeDtypeStruct(shape, rows.dtype),
        in_specs=[pl.BlockSpec((block, width), lambda i: (i, 0))],
        out_specs=pl.BlockSpec((block, *shape[1:]), lambda i: (i, 0, 0, 0)),
        name="split_rows",
    )(rows)


def pick_kernel(cap, relay, group_size, order_ref, start_ref, extra_ref, rows_ref, out_ref, *relay_out):
    last = rows_ref.shape[0] - 1
    unroll = next(u for u in (8, 5, 4, 2, 1) if cap % u == 0)

    def per_dst(j, carry):
        first = start_ref[j]

        def body(b, c):
            for u in range(unroll):
                k = b * unroll + u
                out_ref[j, k] = rows_ref[order_ref[jnp.minimum(first + k, last)]]
            return c

        return lax.fori_loop(0, cap // unroll, body, carry)

    lax.fori_loop(0, group_size, per_dst, 0)
    if relay:

        def per_mid(m, carry):
            for r in range(relay):
                src = jnp.minimum(extra_ref[0] + r * group_size + m, last)
                relay_out[0][m, r] = rows_ref[order_ref[src]]
            return carry

        lax.fori_loop(0, group_size, per_mid, 0)


def pick(order, starts, extra, rows, cap, relay, group_size):
    row = rows.shape[1:]
    outs = [jax.ShapeDtypeStruct((group_size, cap, *row), rows.dtype)]
    if relay:
        outs.append(jax.ShapeDtypeStruct((group_size, relay, *row), rows.dtype))
    return pl.pallas_call(
        functools.partial(pick_kernel, cap, relay, group_size),
        out_shape=outs,
        in_specs=[SMEM, SMEM, SMEM, VMEM],
        out_specs=[VMEM] * len(outs),
        name="pick_rows",
    )(order, starts, extra, rows)


def segment_kernel(start_ref, count_ref, all_ref, out_ref):
    group_size, tiles, _ = all_ref.shape
    lane = lax.broadcasted_iota(jnp.int32, (1, LANES), 1)
    for i in range(group_size):
        s = start_ref[i]
        t = s // LANES
        off = s - t * LANES
        t = jnp.minimum(t, tiles - 1)
        a = all_ref[i, pl.ds(t, 1), :]
        b = all_ref[i, pl.ds(jnp.minimum(t + 1, tiles - 1), 1), :]
        shift = lax.rem(LANES - off, LANES)
        a = pltpu.roll(a, shift, 1)
        b = pltpu.roll(b, shift, 1)
        v = jnp.where(lane < LANES - off, a, b)
        out_ref[pl.ds(i, 1), :] = jnp.where(lane < count_ref[i], v, PAD_KEY)


def segments(starts, counts, all_keys):
    group_size = all_keys.shape[0]
    return pl.pallas_call(
        segment_kernel,
        out_shape=jax.ShapeDtypeStruct((group_size, LANES), all_keys.dtype),
        in_specs=[SMEM, SMEM, VMEM],
        out_specs=VMEM,
        name="segments",
    )(starts, counts, all_keys)


def swap_kernel(src_ref, in_ref, out_ref):
    for j in range(out_ref.shape[0]):
        out_ref[j] = in_ref[src_ref[j]]


def swap(src, blocks):
    return pl.pallas_call(
        swap_kernel,
        out_shape=jax.ShapeDtypeStruct(blocks.shape, blocks.dtype),
        in_specs=[SMEM, VMEM],
        out_specs=VMEM,
        name="swap",
    )(src, blocks)


def place_kernel(n_in, idx_ref, count_ref, *refs):
    ins, (out_ref, held, sem) = refs[:n_in], refs[n_in:]
    step = pl.program_id(0)
    block, width = out_ref.shape
    parts, sub, lanes = held.shape[1:]

    @pl.when(step == 0)
    def _():
        copies = []
        first = 0
        for i, ref in enumerate(ins):
            copies.append(pltpu.make_async_copy(ref, held.at[pl.ds(first, ref.shape[0])], sem.at[i]))
            copies[-1].start()
            first += ref.shape[0]
        held[first] = jnp.zeros(held.shape[1:], held.dtype)
        for c in copies:
            c.wait()

    live = step * block < count_ref[0]

    @pl.when(live)
    def _():
        def body(g, carry):
            r = pl.multiple_of(g * 16, 16)
            rows = []
            for u in range(16):
                k = idx_ref[step * block + r + u]
                rows.append(jnp.concatenate([held[k, q] for q in range(parts)], 0))
            out_ref[pl.ds(r, 16), :] = jnp.stack(rows, 0).reshape(16, width)
            return carry

        lax.fori_loop(0, block // 16, body, 0)

    @pl.when(jnp.logical_not(live))
    def _():
        out_ref[...] = jnp.zeros(out_ref.shape, out_ref.dtype)


def place(idx, count, ins, width):
    n_out = idx.shape[0]
    block = 256
    total = sum(x.shape[0] for x in ins)
    return pl.pallas_call(
        functools.partial(place_kernel, len(ins)),
        grid_spec=pltpu.PrefetchScalarGridSpec(
            num_scalar_prefetch=2,
            grid=(n_out // block,),
            in_specs=[ANY] * len(ins),
            out_specs=pl.BlockSpec((block, width), lambda i, *_: (i, 0)),
            scratch_shapes=[pltpu.VMEM((total + 1, *ins[0].shape[1:]), ins[0].dtype), pltpu.SemaphoreType.DMA((len(ins),))],
        ),
        out_shape=jax.ShapeDtypeStruct((n_out, width), ins[0].dtype),
        name="place_rows",
    )(idx, count, *ins)


def solution(mesh):
    group_size = mesh.shape["g"]

    def local_part(keys_loc, rows_loc):
        n_dev = keys_loc.shape[0]
        width = rows_loc.shape[1]
        cap_rows = 2 * n_dev // group_size
        me = lax.axis_index("g")
        sorted_keys, order = lax.sort((keys_loc, lax.iota(jnp.int32, n_dev)), num_keys=1)
        all_keys = share_keys(sorted_keys.reshape(n_dev // LANES, LANES), group_size)
        rows = split_rows(rows_loc)
        per_sample = n_dev // group_size
        flat_keys = all_keys.reshape(group_size, n_dev)
        all_samples = jnp.sort(flat_keys[:, ::per_sample].reshape(-1))
        splitters = all_samples[group_size + group_size // 2 :: group_size]
        below = (all_keys[:, None] < splitters[None, :, None, None]).astype(jnp.int32)
        edges = jnp.sum(below, axis=(2, 3))
        edges = jnp.concatenate([jnp.zeros((group_size, 1), jnp.int32), edges, jnp.full((group_size, 1), n_dev, jnp.int32)], axis=1)
        counts = edges[:, 1:] - edges[:, :-1]
        over = jnp.maximum(counts - BASE, 0)
        has = (over > 0).astype(jnp.int32)
        short = (jnp.max(jnp.sum(has, 0)) <= 1) & (jnp.max(jnp.sum(has, 1)) <= 1) & (jnp.max(over) <= RELAY * group_size)

        starts = edges[me, :group_size]
        col = lambda m: lax.dynamic_slice_in_dim(m, me, 1, axis=1)[:, 0]
        my_counts = col(counts)
        segs = segments(col(edges), my_counts, all_keys)
        own_count = jnp.sum(my_counts).reshape(1)
        src = lax.broadcasted_iota(jnp.int32, segs.shape, 0)
        pos = lax.broadcasted_iota(jnp.int32, segs.shape, 1)

        def merge(slot, n_slots):
            slot = jnp.where(pos < my_counts[:, None], slot, n_slots)
            return lax.sort((segs.reshape(-1), slot.reshape(-1)), num_keys=1)

        def send(blocks):
            return lax.all_to_all(blocks, "g", 0, 0, tiled=True)

        def flat(blocks):
            return blocks.reshape(-1, *blocks.shape[2:])

        def with_relay():
            dst = jnp.argmax(over[me]).astype(jnp.int32)
            extra = (starts[dst] + BASE).reshape(1)
            base, first = pick(order, starts, extra, rows, BASE, RELAY, group_size)
            first = send(first)
            second = send(swap(jnp.argmax(over, axis=0).astype(jnp.int32), first))
            base = send(base)
            past = pos - BASE
            slot = jnp.where(past < 0, src * BASE + pos, group_size * BASE + lax.rem(past, group_size) * RELAY + past // group_size)
            merged, idx = merge(slot, group_size * (BASE + RELAY))
            return merged, place(idx, own_count, [flat(base), flat(second)], width)

        def direct():
            (base,) = pick(order, starts, jnp.zeros((1,), jnp.int32), rows, cap_rows, 0, group_size)
            base = send(base)
            merged, idx = merge(src * cap_rows + pos, group_size * cap_rows)
            return merged, place(idx, own_count, [flat(base)], width)

        merged, merged_rows = lax.cond(short, with_relay, direct)
        return merged, merged_rows, own_count

    row_spec = P(("batch", "g"))
    mat_spec = P(("batch", "g"), None)
    return jax.shard_map(local_part, mesh=mesh, in_specs=(row_spec, mat_spec), out_specs=(row_spec, mat_spec, row_spec), check_vma=False)
```

time: 370 us -> 210 us (0.57)
  local copies, waits for them, and re-layouts: 115 us -> 2.86 us
  waiting for transfers between devices: 165 us -> 85.3 us
  Pallas kernels: 0 us -> 53.8 us
  blocking collectives: 46.5 us -> 11.5 us
  other arithmetic: 28.7 us -> 39.6 us
    gather x16 -> x0, local copies, waits for them, and re-layouts: 115 us -> none  [the longest x1 31.4 us: local_part(): merged_rows = recv_rows.reshape(-1, width)[merge_order]]
    all_to_all x2, waiting for transfers between devices: 165 us -> 85.3 us  [send(): return lax.all_to_all(blocks, 'g', 0, 0, tiled=True)]
    pallas_call x0 -> x6, Pallas kernels: none -> 53.8 us  [the longest x1 14.7 us: place(): pl.pallas_call(functools.partial(place_kernel, len(ins)), grid_spec=pltpu...]
    unnamed x1 -> x0, blocking collectives: 46.5 us -> none
    reduce_sum x1 -> x3, other arithmetic: 0.63 us -> 20.2 us  [the longest x1 18.8 us: local_part(): edges = jnp.sum(below, axis=(2, 3))]
    select_n x26 -> x0, other arithmetic: 11.7 us -> none  [the longest x1 10.7 us: local_part(): jnp.where(is_valid[:, :, None], rows_loc[sort_order[src_pos]], 0.0)]
    all_to_all x0 -> x1, blocking collectives: none -> 11.5 us  [send(): return lax.all_to_all(blocks, 'g', 0, 0, tiled=True)]
  transfers between devices with their start and end apart: 2 -> 2, of which waited for: 1 -> 2; matrix products, arithmetic and copies ran while one was open for 19% -> 3% of each run, Pallas kernels for 0% -> 0%
where the time goes in v1:
time: 210 us; the launch traced here: 209 us
  waiting for transfers between devices  85.3 us (41%)
  Pallas kernels  53.8 us (26%)
  other arithmetic  39.6 us (19%)
  blocking collectives  11.5 us (5%)
  starting transfers between devices  10.6 us (5%)
  local copies, waits for them, and re-layouts  2.86 us (1%)
  between operations  2.8 us (1%)
  loops' own time  2.62 us (1%)
    all_to_all x2, waiting for transfers between devices, send(): return lax.all_to_all(blocks, 'g', 0, 0, tiled=True)  85.3 us
    reduce_sum x1, other arithmetic, local_part(): edges = jnp.sum(below, axis=(2, 3))  18.8 us
    pallas_call x1, Pallas kernels, place(): pl.pallas_call(functools.partial(place_kernel, len(ins)), grid_spec=pltpu...  14.7 us
    pallas_call x1, Pallas kernels, share_keys(): pl.pallas_call(functools.partial(share_keys_kernel, group_size), out_shap...  14 us
    pallas_call x1, Pallas kernels, pick(): pl.pallas_call(functools.partial(pick_kernel, cap, relay, group_size), ou...  13.1 us
    all_to_all x1, blocking collectives, send(): return lax.all_to_all(blocks, 'g', 0, 0, tiled=True)  11.5 us
    all_to_all x2, starting transfers between devices, send(): return lax.all_to_all(blocks, 'g', 0, 0, tiled=True)  10.6 us
    pallas_call x1, Pallas kernels, split_rows(): pl.pallas_call(split_rows_kernel, grid=(n // block,), out_shape=jax.Shape...  8.97 us
  transfers between devices with their start and end apart: 2, of which 2 were waited for; matrix products, arithmetic and copies ran while one was open for 3% of the time, Pallas kernels for 0%

profile of v1, /device:TPU:103, one launch (start us, length us, event | category | flops | bytes accessed | tf_op | source)
XLA Modules:
  0.0 209.2 jit_solution(18422093621112354968)
XLA Ops:
  0.7 5.9 %sort.76 = (f32[2048]{0:T(1024)}, s32[2048]{0:T(1024)S(1)}) sort(f32[2048]{0:T(1024)} %param.4, s32[2048]{0:T(1024)S(1)} %iota.41), dimensions={0}, to_apply=%region_0.0 | sort | flops 22528 | bytes 32768 | tf_op jit(solution)/shard_map/sort | solution.py:233
  6.7 14.0 %share_keys.1.all_ref = f32[32,16,128]{2,1,0:T(8,128)} custom-call(f32[16,128]{1,0:T(8,128)} %bitcast.28), custom_call_target="tpu_custom_call" | custom-call | tf_op jit(solution)/shard_map/share_keys/pallas_call | solution.py:46
  20.7 1.0 copy.13
  22.0 4.5 %sort.77 = (f32[1024]{0:T(1024)S(1)}, s32[1024]{0:T(1024)}) sort(f32[1024]{0:T(1024)S(1)} %reshape.47, s32[1024]{0:T(1024)S(1)} %iota.42), dimensions={0}, to_apply=%region_1.0 | sort | flops 10240 | bytes 16384 | tf_op jit(solution)/shard_map/jit(sort)/sort | solution.py:238
  26.7 18.8 %convert_reduce_fusion = s32[32,31]{1,0:T(8,128)S(1)} fusion(f32[32,16,128]{2,1,0:T(8,128)} %share_keys.1.all_ref, f32[31]{0:T(128)S(1)} %slice.11), kind=kLoop, calls=%fused_computation.14 | loop fusion | flops 6093856 | bytes 266236 | tf_op jit(solution)/shard_map/reduce_sum | solution.py:241
  45.5 0.8 fusion.10
  46.3 1.3 segments.1
  47.6 0.7 convert_reduce_fusion.1
  49.0 0.6 reduce_max.27
  50.3 0.6 reduce_max.28
  51.6 9.0 %split_rows.1 = bf16[2048,3,4,128]{3,2,1,0:T(4,128)(2,1)} custom-call(bf16[2048,1536]{1,0:T(8,128)(2,1)} %rows_ref.1), custom_call_target="tpu_custom_call" | custom-call | tf_op jit(solution)/shard_map/split_rows/pallas_call | solution.py:75
  60.5 148.5 %conditional.1 = (f32[4096]{0:T(1024)}, bf16[4096,1536]{1,0:T(8,128)(2,1)}) conditional(s32[]{:T(128)} %convert_element_type.11, (f32[32,128]{1,0:T(8,128)S(1)}, s32[32,1]{1,0:T(8,128)S(1)}, s32[32,128]{1,0:T(8,128)S(1)}, s32[32,128]{1,0:T(8,128)S(1)}, s32[32,128]{1,0:T(8,128)S(1)}, /*index=5*/s32[2048]{0:T(1024)S(1)}, s32[32]{0:T(128)S(1)}, ...), branch_computations={%region_9.11_spmd, %region_11.15_spmd} | conditional | flops 154624 | bytes 37929392 | solution.py:284
  60.5 0.7 bitcast_reduce_fusion
  63.1 0.6 dynamic_slice.11
  64.4 13.1 %pick_rows.3 = (bf16[32,65,3,4,128]{4,3,2,1,0:T(4,128)(2,1)}, bf16[32,2,3,4,128]{4,3,2,1,0:T(4,128)(2,1)}) custom-call(s32[2048]{0:T(1024)S(1)} %get-tuple-element.62.order_ref, s32[32]{0:T(128)S(1)} %get-tuple-element.63.start_ref, s32[1]{0:T(128)S(6)} %add.29.extra_ref, bf16[2048,3,4,128]{3,2,1,0:T(4,128)(2,1)} %get-tuple-element.67.rows_ref), custom_call_target="tpu_custom_call" | custom-call | tf_op jit(solution)/shard_map/cond/branch_1_fun/pick_rows/pallas_call | solution.py:117
  77.5 5.4 %all-to-all-start.2 = ((bf16[32,2,3,4,128]{4,3,2,1,0:T(4,128)(2,1)}), bf16[32,2,3,4,128]{4,3,2,1,0:T(4,128)(2,1)S(1)}, u32[]{:S(2)}, u32[]{:S(2)}) async-start(bf16[32,2,3,4,128]{4,3,2,1,0:T(4,128)(2,1)} %get-tuple-element.70), calls=%async_computation.2 | async-start | bytes 393216 | tf_op jit(solution)/shard_map/cond/branch_1_fun/all_to_all | solution.py:261
  83.4 5.8 %all-to-all-done.2.in_ref = bf16[32,2,3,4,128]{4,3,2,1,0:T(4,128)(2,1)S(1)} async-done(((bf16[32,2,3,4,128]{4,3,2,1,0:T(4,128)(2,1)}), bf16[32,2,3,4,128]{4,3,2,1,0:T(4,128)(2,1)S(1)}, u32[]{:S(2)}, u32[]{:S(2)}) %all-to-all-start.2) | async-done | bytes 196640 | tf_op jit(solution)/shard_map/cond/branch_1_fun/all_to_all | solution.py:261
  89.2 0.7 copy-done
  89.9 1.6 swap.1
  91.5 11.5 %all_to_all.16 = bf16[32,2,3,4,128]{4,3,2,1,0:T(4,128)(2,1)} all-to-all(bf16[32,2,3,4,128]{4,3,2,1,0:T(4,128)(2,1)} %swap.1), channel_id=1, replica_groups=mesh['batch'=1,'g'=32] {'g'}, dimensions={0} | all-to-all | bytes 393216 | tf_op jit(solution)/shard_map/cond/branch_1_fun/all_to_all | solution.py:261
  103.0 5.3 %all-to-all-start.1 = ((bf16[32,65,3,4,128]{4,3,2,1,0:T(4,128)(2,1)}), bf16[32,65,3,4,128]{4,3,2,1,0:T(4,128)(2,1)}, u32[]{:S(2)}, u32[]{:S(2)}) async-start(bf16[32,65,3,4,128]{4,3,2,1,0:T(4,128)(2,1)} %get-tuple-element.68), calls=%async_computation.1 | async-start | bytes 12779520 | tf_op jit(solution)/shard_map/cond/branch_1_fun/all_to_all | solution.py:261
  108.5 6.3 %sort.73 = (f32[4096]{0:T(1024)}, s32[4096]{0:T(1024)}, s32[4096]{0:T(1024)}) sort(f32[4096]{0:T(1024)S(1)} %bitcast.27, s32[4096]{0:T(1024)S(1)} %fusion.3, s32[4096]{0:T(1024)S(1)} %iota.30), dimensions={0}, to_apply=%region_12.12 | sort | flops 49152 | bytes 98304 | tf_op jit(solution)/shard_map/cond/branch_1_fun/sort | solution.py:258
  114.8 79.6 %all-to-all-done.1 = bf16[32,65,3,4,128]{4,3,2,1,0:T(4,128)(2,1)} async-done(((bf16[32,65,3,4,128]{4,3,2,1,0:T(4,128)(2,1)}), bf16[32,65,3,4,128]{4,3,2,1,0:T(4,128)(2,1)}, u32[]{:S(2)}, u32[]{:S(2)}) %all-to-all-start.1) | async-done | bytes 6389792 | tf_op jit(solution)/shard_map/cond/branch_1_fun/all_to_all | solution.py:261
  194.3 14.7 %place_rows.3 = bf16[4096,1536]{1,0:T(8,128)(2,1)} custom-call(s32[4096]{0:T(1024)} %get-tuple-element.60.idx_ref, s32[1]{0:T(128)} %get-tuple-element.61.count_ref, bf16[2080,3,4,128]{3,2,1,0:T(4,128)(2,1)} %bitcast.8.refs_0_, bf16[64,3,4,128]{3,2,1,0:T(4,128)(2,1)} %bitcast.24), custom_call_target="tpu_custom_call" | custom-call | tf_op jit(solution)/shard_map/cond/branch_1_fun/place_rows/pallas_call | solution.py:211
  (18 shorter events, 1.3 us)
Async XLA Ops:
  77.5 11.7 %all-to-all-start.2 = ((bf16[32,2,3,4,128]{4,3,2,1,0:T(4,128)(2,1)}), bf16[32,2,3,4,128]{4,3,2,1,0:T(4,128)(2,1)S(1)}, u32[]{:S(2)}, u32[]{:S(2)}) async-start(bf16[32,2,3,4,128]{4,3,2,1,0:T(4,128)(2,1)} %get-tuple-element.70), calls=%async_computation.2 | async-start | bytes 393216 | tf_op jit(solution)/shard_map/cond/branch_1_fun/all_to_all | solution.py:261
  89.2 0.7 copy-start
  103.0 91.3 %all-to-all-start.1 = ((bf16[32,65,3,4,128]{4,3,2,1,0:T(4,128)(2,1)}), bf16[32,65,3,4,128]{4,3,2,1,0:T(4,128)(2,1)}, u32[]{:S(2)}, u32[]{:S(2)}) async-start(bf16[32,65,3,4,128]{4,3,2,1,0:T(4,128)(2,1)} %get-tuple-element.68), calls=%async_computation.1 | async-start | bytes 12779520 | tf_op jit(solution)/shard_map/cond/branch_1_fun/all_to_all | solution.py:261

commit v2 on v0

v2 whole, which is shorter than its diff:
```python
import functools

import jax
import jax.numpy as jnp
from jax import lax
from jax.experimental import pallas as pl
from jax.experimental.pallas import tpu as pltpu
from jax.sharding import PartitionSpec as P

PAD_KEY = 128.0
LANES = 128
SUB = 4
BASE = 65
RELAY = 2

VMEM = pl.BlockSpec(memory_space=pltpu.VMEM)
SMEM = pl.BlockSpec(memory_space=pltpu.SMEM)
ANY = pl.BlockSpec(memory_space=pl.ANY)
MESH = pl.DeviceIdType.MESH
STARTS, COL_STARTS, COL_COUNTS, FROM_SRC, EXTRA, SHORT, OWN = range(7)


def share_keys_kernel(group_size, block, keys_ref, rows_ref, all_ref, split_ref, fetched, held, send_sem, recv_sem, in_sem, out_sem):
    me = lax.axis_index("g")
    barrier = pltpu.get_barrier_semaphore()
    for d in range(1, group_size):
        pl.semaphore_signal(barrier, inc=1, device_id={"g": lax.rem(me + d, group_size)}, device_id_type=MESH)
    n, width = rows_ref.shape
    steps = n // block
    tiles = width // LANES

    def fetch(s):
        return pltpu.make_async_copy(rows_ref.at[pl.ds(s * block, block)], fetched.at[s], in_sem.at[s])

    def keep(s):
        return pltpu.make_async_copy(held.at[s], split_ref.at[pl.ds(s * block, block)], out_sem.at[s])

    for s in range(steps):
        fetch(s).start()
    pl.semaphore_wait(barrier, group_size - 1)
    copies = []
    for d in range(1, group_size):
        copies.append(
            pltpu.make_async_remote_copy(
                src_ref=keys_ref,
                dst_ref=all_ref.at[me],
                send_sem=send_sem.at[d],
                recv_sem=recv_sem.at[d],
                device_id={"g": lax.rem(me + d, group_size)},
                device_id_type=MESH,
            )
        )
        copies[-1].start()
    all_ref[pl.ds(me, 1)] = keys_ref[...][None]
    for s in range(steps):
        fetch(s).wait()

        def body(g, carry):
            r = pl.multiple_of(g * 16, 16)
            v = fetched[s, pl.ds(r, 16), :].reshape(16, tiles, LANES)
            for q in range(tiles // SUB):
                held[s, pl.ds(r, 16), q] = v[:, SUB * q : SUB * (q + 1)]
            return carry

        lax.fori_loop(0, block // 16, body, 0)
        if s:
            keep(s - 1).start()
    for c in copies:
        c.wait()
    keep(steps - 1).start()
    for s in range(steps):
        keep(s).wait()


def share_keys(keys, rows, group_size):
    n, width = rows.shape
    block = 512
    row = (width // (SUB * LANES), SUB, LANES)
    return pl.pallas_call(
        functools.partial(share_keys_kernel, group_size, block),
        out_shape=[
            jax.ShapeDtypeStruct((group_size, *keys.shape), keys.dtype),
            jax.ShapeDtypeStruct((n, *row), rows.dtype),
        ],
        in_specs=[VMEM, ANY],
        out_specs=[VMEM, ANY],
        scratch_shapes=[
            pltpu.VMEM((n // block, block, width), rows.dtype),
            pltpu.VMEM((n // block, block, *row), rows.dtype),
            pltpu.SemaphoreType.DMA((group_size,)),
            pltpu.SemaphoreType.DMA((group_size,)),
            pltpu.SemaphoreType.DMA((n // block,)),
            pltpu.SemaphoreType.DMA((n // block,)),
        ],
        compiler_params=pltpu.CompilerParams(collective_id=0, has_side_effects=True),
        name="share_keys",
    )(keys, rows)


def plan_kernel(cap, most, all_ref, table_ref, edge_ref):
    group_size, tiles, _ = all_ref.shape
    n_dev = tiles * LANES
    per = n_dev // group_size
    each = LANES // per
    me = lax.axis_index("g")
    f32 = jnp.float32
    lane = lax.broadcasted_iota(jnp.int32, (tiles, LANES), 1)
    sub = lax.broadcasted_iota(jnp.int32, (tiles, LANES), 0)
    group_lane = lax.broadcasted_iota(jnp.int32, (group_size, LANES), 1)
    group_sub = lax.broadcasted_iota(jnp.int32, (group_size, LANES), 0)

    def samples(i):
        return [jnp.broadcast_to(all_ref[i, :, l * per : l * per + 1], (tiles, LANES)) for l in range(each)]

    fit = LANES // group_size
    packed = []
    for c in range(group_size // fit):
        acc = jnp.zeros((tiles, LANES), f32)
        for i in range(c * fit, (c + 1) * fit):
            for l, a in enumerate(samples(i)):
                acc = jnp.where(lane == (i % fit) * group_size + each * sub + l, a, acc)
        packed.append(jnp.sum(acc, axis=0, keepdims=True))
    target = lax.broadcasted_iota(jnp.int32, (1, LANES), 1) * group_size + group_size // 2
    target = jnp.where((target > group_size) & (target < group_size * group_size), target, -1).astype(f32)
    found = jnp.zeros((tiles, LANES), f32)
    for i in range(group_size):
        for a in samples(i):
            less = jnp.zeros((tiles, LANES), f32)
            for b in packed:
                less += (b < a).astype(f32)
            rank = jnp.sum(less, axis=1, keepdims=True)
            found += jnp.where(rank == target, a, 0.0)
    splitters = jnp.sum(found, axis=0, keepdims=True)
    splitters = jnp.sum(jnp.where(group_lane == group_sub, splitters, 0.0), axis=1, keepdims=True)
    splitters = jnp.where(group_sub == 0, -PAD_KEY, splitters)

    edge_ref[...] = jnp.zeros(edge_ref.shape, f32)

    def count(b, carry):
        edges = edge_ref[...]
        for u in range(4):
            i = b * 4 + u
            less = jnp.zeros((group_size, LANES), f32)
            for r in range(tiles):
                less += (all_ref[i, r : r + 1, :] < splitters).astype(f32)
            edges = jnp.where(group_lane == i, jnp.sum(less, axis=1, keepdims=True), edges)
        edge_ref[...] = edges
        return carry

    lax.fori_loop(0, group_size // 4, count, 0)
    edges = edge_ref[...]
    after = jnp.concatenate([edges[1:], jnp.full((1, LANES), n_dev, f32)], 0)
    counts = jnp.where(group_lane < group_size, after - edges, 0.0)
    over = jnp.maximum(counts - cap, 0.0)
    has = (over > 0).astype(f32)
    worst = jnp.maximum(jnp.max(jnp.sum(has, axis=0, keepdims=True), axis=1, keepdims=True), jnp.max(jnp.sum(has, axis=1, keepdims=True), axis=0, keepdims=True))
    most_over = jnp.max(jnp.max(over, axis=0, keepdims=True), axis=1, keepdims=True)
    short = ((worst <= 1) & (most_over <= most)).astype(f32)

    def to_row(column):
        return jnp.sum(jnp.where(group_lane == group_sub, column, 0.0), axis=0, keepdims=True)

    mine = group_lane == me
    starts = to_row(jnp.sum(jnp.where(mine, edges, 0.0), axis=1, keepdims=True))
    col_starts = jnp.sum(jnp.where(group_sub == me, edges, 0.0), axis=0, keepdims=True)
    col_counts = jnp.sum(jnp.where(group_sub == me, counts, 0.0), axis=0, keepdims=True)
    from_src = to_row(jnp.sum(has * group_lane.astype(f32), axis=1, keepdims=True))
    extra = jnp.sum(jnp.sum(jnp.where(mine, has * (edges + cap), 0.0), axis=0, keepdims=True), axis=1, keepdims=True)
    own = jnp.sum(col_counts, axis=1, keepdims=True)
    rows = [starts, col_starts, col_counts, from_src, extra, short, own, own]
    table_ref[...] = jnp.concatenate([jnp.broadcast_to(r, (1, LANES)) for r in rows], 0).astype(jnp.int32)


def plan(all_keys, cap, most):
    return pl.pallas_call(
        functools.partial(plan_kernel, cap, most),
        out_shape=jax.ShapeDtypeStruct((8, LANES), jnp.int32),
        in_specs=[VMEM],
        out_specs=VMEM,
        scratch_shapes=[pltpu.VMEM((all_keys.shape[0], LANES), jnp.float32)],
        name="plan",
    )(all_keys)


def segment_kernel(cap, relay, table_ref, all_ref, out_ref, slot_ref):
    group_size, tiles, _ = all_ref.shape
    lane = lax.broadcasted_iota(jnp.int32, (1, LANES), 1)
    short = table_ref[SHORT, 0] > 0
    past = lane - cap
    relayed = group_size * cap + lax.rem(past, group_size) * relay + past // group_size
    unused = jnp.where(short, group_size * (cap + relay), group_size * LANES)
    for i in range(group_size):
        s = table_ref[COL_STARTS, i]
        t = s // LANES
        off = s - t * LANES
        t = jnp.minimum(t, tiles - 1)
        a = all_ref[i, pl.ds(t, 1), :]
        b = all_ref[i, pl.ds(jnp.minimum(t + 1, tiles - 1), 1), :]
        shift = lax.rem(LANES - off, LANES)
        a = pltpu.roll(a, shift, 1)
        b = pltpu.roll(b, shift, 1)
        v = jnp.where(lane < LANES - off, a, b)
        live = lane < table_ref[COL_COUNTS, i]
        out_ref[pl.ds(i, 1), :] = jnp.where(live, v, PAD_KEY)
        slot = jnp.where(short, jnp.where(past < 0, i * cap + lane, relayed), i * LANES + lane)
        slot_ref[pl.ds(i, 1), :] = jnp.where(live, slot, unused)


def segments(table, all_keys, cap, relay):
    shape = (all_keys.shape[0], LANES)
    return pl.pallas_call(
        functools.partial(segment_kernel, cap, relay),
        out_shape=[jax.ShapeDtypeStruct(shape, all_keys.dtype), jax.ShapeDtypeStruct(shape, jnp.int32)],
        in_specs=[SMEM, VMEM],
        out_specs=[VMEM, VMEM],
        name="segments",
    )(table, all_keys)


def exchange_kernel(group_size, cap, relay, early, order_ref, table_ref, rows_ref, out_ref, held, outgoing, first, arrived, second, load_sem, own_sem, send_sem, recv_sem):
    me = lax.axis_index("g")
    last = rows_ref.shape[0] - 1
    load = pltpu.make_async_copy(rows_ref, held, load_sem)
    load.start()
    barrier = pltpu.get_barrier_semaphore()
    for d in range(1, group_size):
        pl.semaphore_signal(barrier, inc=1, device_id={"g": lax.rem(me + d, group_size)}, device_id_type=MESH)

    def peer(d):
        return lax.rem(me + d, group_size)

    def remote(d, src, dst, kind):
        return pltpu.make_async_remote_copy(
            src_ref=src, dst_ref=dst, send_sem=send_sem.at[kind, d], recv_sem=recv_sem.at[kind, d], device_id={"g": peer(d)}, device_id_type=MESH
        )

    def base(d):
        return remote(d, outgoing.at[peer(d)], out_ref.at[pl.ds(me * cap, cap)], 0)

    def hop_one(d):
        return remote(d, first.at[peer(d)], arrived.at[me], 1)

    def hop_two(d):
        return remote(d, second.at[peer(d)], out_ref.at[pl.ds(group_size * cap + me * relay, relay)], 2)

    own_base = pltpu.make_async_copy(outgoing.at[me], out_ref.at[pl.ds(me * cap, cap)], own_sem.at[0])
    own_two = pltpu.make_async_copy(second.at[me], out_ref.at[pl.ds(group_size * cap + me * relay, relay)], own_sem.at[1])

    def gather(d):
        dst = peer(d)
        begin = table_ref[STARTS, dst]

        def body(b, carry):
            for u in range(5):
                k = b * 5 + u
                outgoing[dst, k] = held[order_ref[jnp.minimum(begin + k, last)]]
            return carry

        lax.fori_loop(0, cap // 5, body, 0)

    load.wait()
    extra = table_ref[EXTRA, 0]

    def gather_extra(m, carry):
        for r in range(relay):
            first[m, r] = held[order_ref[jnp.minimum(extra + r * group_size + m, last)]]
        return carry

    lax.fori_loop(0, group_size, gather_extra, 0)
    arrived[pl.ds(me, 1)] = first[pl.ds(me, 1)]
    gather(1)
    pl.semaphore_wait(barrier, group_size - 1)

    def start_one(d, carry):
        hop_one(d).start()
        return carry

    lax.fori_loop(1, group_size, start_one, 0)

    def step(d, carry):
        gather(d)
        base(d - 1).start()
        return carry

    lax.fori_loop(2, early, step, 0)

    def wait_one(d, carry):
        hop_one(d).wait()
        return carry

    lax.fori_loop(1, group_size, wait_one, 0)
    for j in range(group_size):
        second[j] = arrived[table_ref[FROM_SRC, j]]
    lax.fori_loop(early, early + 1, step, 0)

    def start_two(d, carry):
        hop_two(d).start()
        return carry

    lax.fori_loop(1, group_size, start_two, 0)
    lax.fori_loop(early + 1, group_size, step, 0)
    gather(0)
    base(group_size - 1).start()
    own_two.start()
    own_base.start()

    def wait_rest(d, carry):
        hop_two(d).wait()
        base(d).wait()
        return carry

    lax.fori_loop(1, group_size, wait_rest, 0)
    own_two.wait()
    own_base.wait()


def exchange(order, table, rows, cap, relay, group_size):
    row = rows.shape[1:]
    return pl.pallas_call(
        functools.partial(exchange_kernel, group_size, cap, relay, 9),
        out_shape=jax.ShapeDtypeStruct((group_size * (cap + relay), *row), rows.dtype),
        in_specs=[SMEM, SMEM, ANY],
        out_specs=ANY,
        scratch_shapes=[
            pltpu.VMEM(rows.shape, rows.dtype),
            pltpu.VMEM((group_size, cap, *row), rows.dtype),
            pltpu.VMEM((group_size, relay, *row), rows.dtype),
            pltpu.VMEM((group_size, relay, *row), rows.dtype),
            pltpu.VMEM((group_size, relay, *row), rows.dtype),
            pltpu.SemaphoreType.DMA,
            pltpu.SemaphoreType.DMA((2,)),
            pltpu.SemaphoreType.DMA((3, group_size)),
            pltpu.SemaphoreType.DMA((3, group_size)),
        ],
        compiler_params=pltpu.CompilerParams(collective_id=1, has_side_effects=True),
        name="exchange",
    )(order, table, rows)


def pick_kernel(cap, group_size, order_ref, table_ref, rows_ref, out_ref):
    last = rows_ref.shape[0] - 1

    def per_dst(j, carry):
        first = table_ref[STARTS, j]

        def body(b, c):
            for u in range(8):
                k = b * 8 + u
                out_ref[j, k] = rows_ref[order_ref[jnp.minimum(first + k, last)]]
            return c

        return lax.fori_loop(0, cap // 8, body, carry)

    lax.fori_loop(0, group_size, per_dst, 0)


def pick(order, table, rows, cap, group_size):
    return pl.pallas_call(
        functools.partial(pick_kernel, cap, group_size),
        out_shape=jax.ShapeDtypeStruct((group_size, cap, *rows.shape[1:]), rows.dtype),
        in_specs=[SMEM, SMEM, VMEM],
        out_specs=VMEM,
        name="pick_rows",
    )(order, table, rows)


def place_kernel(idx_ref, count_ref, in_ref, out_ref, held, staged, blank, in_sem, out_sem, blank_sem):
    slots, block, width = staged.shape
    total = in_ref.shape[0]
    parts = held.shape[1]
    load = pltpu.make_async_copy(in_ref, held.at[pl.ds(0, total)], in_sem)
    load.start()
    blank[...] = jnp.zeros(blank.shape, blank.dtype)
    held[total] = jnp.zeros(held.shape[1:], held.dtype)
    steps = out_ref.shape[0] // block
    live = pl.cdiv(count_ref[0], block)

    def clear(s):
        return pltpu.make_async_copy(blank, out_ref.at[pl.ds(s * block, block)], blank_sem)

    def store(s):
        slot = lax.rem(s, slots)
        return pltpu.make_async_copy(staged.at[slot], out_ref.at[pl.ds(s * block, block)], out_sem.at[slot])

    load.wait()

    def start_clear(s, carry):
        clear(s).start()
        return carry

    lax.fori_loop(live, steps, start_clear, 0)

    def step(s, carry):
        @pl.when(s >= slots)
        def _():
            store(s - slots).wait()

        slot = lax.rem(s, slots)

        def body(g, c):
            r = pl.multiple_of(g * 16, 16)
            rows = []
            for u in range(16):
                k = idx_ref[s * block + r + u]
                rows.append(jnp.concatenate([held[k, q] for q in range(parts)], 0))
            staged[slot, pl.ds(r, 16), :] = jnp.stack(rows, 0).reshape(16, width)
            return c

        lax.fori_loop(0, block // 16, body, 0)
        store(s).start()
        return carry

    lax.fori_loop(0, live, step, 0)

    def end_store(s, carry):
        store(s).wait()
        return carry

    lax.fori_loop(jnp.maximum(live - slots, 0), live, end_store, 0)

    def end_clear(s, carry):
        clear(s).wait()
        return carry

    lax.fori_loop(live, steps, end_clear, 0)


def place(idx, count, rows, width):
    n_out = idx.shape[0]
    block, slots = 128, 4
    return pl.pallas_call(
        place_kernel,
        out_shape=jax.ShapeDtypeStruct((n_out, width), rows.dtype),
        in_specs=[SMEM, SMEM, ANY],
        out_specs=ANY,
        scratch_shapes=[
            pltpu.VMEM((rows.shape[0] + 1, *rows.shape[1:]), rows.dtype),
            pltpu.VMEM((slots, block, width), rows.dtype),
            pltpu.VMEM((block, width), rows.dtype),
            pltpu.SemaphoreType.DMA,
            pltpu.SemaphoreType.DMA((slots,)),
            pltpu.SemaphoreType.DMA,
        ],
        name="place_rows",
    )(idx, count, rows)


def solution(mesh):
    group_size = mesh.shape["g"]

    def local_part(keys_loc, rows_loc):
        n_dev = keys_loc.shape[0]
        width = rows_loc.shape[1]
        cap_rows = 2 * n_dev // group_size
        sorted_keys, order = lax.sort((keys_loc, lax.iota(jnp.int32, n_dev)), num_keys=1)
        all_keys, rows = share_keys(sorted_keys.reshape(n_dev // LANES, LANES), rows_loc, group_size)
        table = plan(all_keys, BASE, RELAY * group_size)
        segs, slots = segments(table, all_keys, BASE, RELAY)
        merged, idx = lax.sort((segs.reshape(-1), slots.reshape(-1)), num_keys=1)
        own_count = table[OWN, :1]

        def with_relay():
            return place(idx, own_count, exchange(order, table, rows, BASE, RELAY, group_size), width)

        def direct():
            blocks = lax.all_to_all(pick(order, table, rows, cap_rows, group_size), "g", 0, 0, tiled=True)
            return place(idx, own_count, blocks.reshape(-1, *blocks.shape[2:]), width)

        merged_rows = lax.cond(table[SHORT, 0] > 0, with_relay, direct)
        return merged, merged_rows, own_count

    row_spec = P(("batch", "g"))
    mat_spec = P(("batch", "g"), None)
    return jax.shard_map(local_part, mesh=mesh, in_specs=(row_spec, mat_spec), out_specs=(row_spec, mat_spec, row_spec), check_vma=False)
```

time: 370 us -> 179 us (0.48)
  the two profiles are of different devices: /device:TPU:103 before, /device:TPU:97 now
where the time goes in v2:
time: 179 us; the launch traced here: 178 us
  Pallas kernels  163 us (91%)
  other arithmetic  12.9 us (7%)
    pallas_call x1, Pallas kernels, exchange(): pl.pallas_call(functools.partial(exchange_kernel, group_size, cap, relay,...  130 us
    pallas_call x1, Pallas kernels, share_keys(): pl.pallas_call(functools.partial(share_keys_kernel, group_size, block), o...  16.8 us
    pallas_call x1, Pallas kernels, place(): pl.pallas_call(place_kernel, out_shape=jax.ShapeDtypeStruct((n_out, width...  11.8 us
    sort x1, other arithmetic, local_part(): merged, idx = lax.sort((segs.reshape(-1), slots.reshape(-1)), num_keys=1)  7.01 us
    sort x1, other arithmetic, local_part(): lax.sort((keys_loc, lax.iota(jnp.int32, n_dev)), num_keys=1)  5.94 us

profile of v2, /device:TPU:97, one launch (start us, length us, event | category | flops | bytes accessed | tf_op | source)
XLA Modules:
  0.0 178.1 jit_solution(5081523349121236391)
XLA Ops:
  0.6 5.9 %sort.38 = (f32[2048]{0:T(1024)}, s32[2048]{0:T(1024)S(1)}) sort(f32[2048]{0:T(1024)} %param.4, s32[2048]{0:T(1024)S(1)} %iota.6), dimensions={0}, to_apply=%region_0.0 | sort | flops 22528 | bytes 32768 | tf_op jit(solution)/shard_map/sort | solution.py:455
  6.6 16.8 %share_keys.1 = (f32[32,16,128]{2,1,0:T(8,128)}, bf16[2048,3,4,128]{3,2,1,0:T(4,128)(2,1)}) custom-call(f32[16,128]{1,0:T(8,128)} %bitcast.9, bf16[2048,1536]{1,0:T(8,128)(2,1)} %rows_ref.1), custom_call_target="tpu_custom_call" | custom-call | tf_op jit(solution)/shard_map/share_keys/pallas_call | solution.py:79
  23.4 3.3 %plan.1.table_ref = s32[8,128]{1,0:T(8,128)S(1)} custom-call(f32[32,16,128]{2,1,0:T(8,128)} %get-tuple-element.47.all_ref), custom_call_target="tpu_custom_call" | custom-call | tf_op jit(solution)/shard_map/plan/pallas_call | solution.py:175
  26.7 1.9 %segments.1 = (f32[32,128]{1,0:T(8,128)}, s32[32,128]{1,0:T(8,128)}) custom-call(s32[8,128]{1,0:T(8,128)S(1)} %plan.1.table_ref, f32[32,16,128]{2,1,0:T(8,128)} %get-tuple-element.47.all_ref), custom_call_target="tpu_custom_call" | custom-call | tf_op jit(solution)/shard_map/segments/pallas_call | solution.py:211
  28.6 7.0 %sort.39 = (f32[4096]{0:T(1024)}, s32[4096]{0:T(1024)S(1)}, s32[4096]{0:T(1024)}) sort(f32[4096]{0:T(1024)} %bitcast.7, s32[4096]{0:T(1024)} %bitcast.8, s32[4096]{0:T(1024)S(1)} %iota.7), dimensions={0}, to_apply=%region_1.0 | sort | flops 49152 | bytes 98304 | tf_op jit(solution)/shard_map/sort | solution.py:459
  35.6 0.5 fusion
  36.8 141.3 %conditional.1 = (bf16[4096,1536]{1,0:T(8,128)(2,1)}) conditional(s32[]{:T(128)} %bitcast.4, (s32[2048]{0:T(1024)S(1)}, s32[8,128]{1,0:T(8,128)S(1)}, bf16[2048,3,4,128]{3,2,1,0:T(4,128)(2,1)}, s32[4096]{0:T(1024)S(1)}, s32[1]{0:T(128)}) %tuple.15, (s32[2048]{0:T(1024)S(1)}, s32[8,128]{1,0:T(8,128)S(1)}, bf16[2048,3,4,128]{3,2,1,0:T(4,128)(2,1)}, ...), branch_computations={%region_2.0_spmd, %region_3.0_spmd} | conditional | bytes 25165832 | solution.py:469
  36.8 129.5 %exchange.1.in_ref = bf16[2144,3,4,128]{3,2,1,0:T(4,128)(2,1)} custom-call(s32[2048]{0:T(1024)S(1)} %get-tuple-element.32.order_ref, s32[8,128]{1,0:T(8,128)S(1)} %get-tuple-element.33.table_ref, bf16[2048,3,4,128]{3,2,1,0:T(4,128)(2,1)} %get-tuple-element.34.rows_ref), custom_call_target="tpu_custom_call" | custom-call | tf_op jit(solution)/shard_map/cond/branch_1_fun/exchange/pallas_call | solution.py:319
  166.4 11.8 %place_rows.3 = bf16[4096,1536]{1,0:T(8,128)(2,1)} custom-call(s32[4096]{0:T(1024)S(1)} %get-tuple-element.30.idx_ref, s32[1]{0:T(128)} %get-tuple-element.31.count_ref, bf16[2144,3,4,128]{3,2,1,0:T(4,128)(2,1)} %exchange.1.in_ref), custom_call_target="tpu_custom_call" | custom-call | tf_op jit(solution)/shard_map/cond/branch_1_fun/place_rows/pallas_call | solution.py:431
  (2 shorter events, 0.0 us)

commit v3 on v2

v3 whole, which is shorter than its diff:
```python
import functools

import jax
import jax.numpy as jnp
from jax import lax
from jax.experimental import pallas as pl
from jax.experimental.pallas import tpu as pltpu
from jax.sharding import PartitionSpec as P

PAD_KEY = 128.0
LANES = 128
SUB = 4
BASE = 65
RELAY = 2
WINDOW = 6
SIDE = 4
CORES = 2
SLOTS = (((0, 2), (2, 0)), ((0, 1), (2, 3)), ((0, 3), (2, 1)), ((1, 0), (3, 2)), ((3, 0), (1, 2)), ((3, 1), (1, 3)), ((3, 3), (1, 1)), ((2, 2),))
STEPS = ((0, 0, 1), *((dx, dy, dc) for slot in SLOTS for dc in (1, 0) for dx, dy in slot))

VMEM = pl.BlockSpec(memory_space=pltpu.VMEM)
SMEM = pl.BlockSpec(memory_space=pltpu.SMEM)
ANY = pl.BlockSpec(memory_space=pl.ANY)
MESH = pl.DeviceIdType.MESH
STARTS, COL_STARTS, COL_COUNTS, FROM_SRC, EXTRA, SHORT, OWN = range(7)


def bitonic_sort(keys, vals):
    rows, lanes = keys.shape
    pos = lax.broadcasted_iota(jnp.int32, keys.shape, 0) * lanes + lax.broadcasted_iota(jnp.int32, keys.shape, 1)

    def partner(x, j, low):
        axis, size, d = (1, lanes, j) if j < lanes else (0, rows, j // lanes)
        return jnp.where(low, pltpu.roll(x, size - d, axis), pltpu.roll(x, d, axis))

    k = 2
    while k <= rows * lanes:
        j = k // 2
        while j:
            low = (pos & j) == 0
            keep_min = jnp.logical_xor(low, (pos & k) != 0)
            other = partner(keys, j, low)
            swap = jnp.logical_or(jnp.logical_and(keep_min, keys > other), jnp.logical_and(jnp.logical_not(keep_min), keys < other))
            vals = jnp.where(swap, partner(vals, j, low), vals)
            keys = jnp.where(swap, other, keys)
            j //= 2
        k *= 2
    return keys, vals


def make_plan(me, cap, most, all_ref, edge_ref):
    group_size, tiles, _ = all_ref.shape
    n_dev = tiles * LANES
    per = n_dev // group_size
    each = LANES // per
    f32 = jnp.float32
    lane = lax.broadcasted_iota(jnp.int32, (tiles, LANES), 1)
    sub = lax.broadcasted_iota(jnp.int32, (tiles, LANES), 0)
    group_lane = lax.broadcasted_iota(jnp.int32, (group_size, LANES), 1)
    group_sub = lax.broadcasted_iota(jnp.int32, (group_size, LANES), 0)

    def samples(i):
        return [jnp.broadcast_to(all_ref[i, :, l * per : l * per + 1], (tiles, LANES)) for l in range(each)]

    fit = LANES // group_size
    packed = []
    for c in range(group_size // fit):
        acc = jnp.zeros((tiles, LANES), f32)
        for i in range(c * fit, (c + 1) * fit):
            for l, a in enumerate(samples(i)):
                acc = jnp.where(lane == (i % fit) * group_size + each * sub + l, a, acc)
        packed.append(jnp.sum(acc, axis=0, keepdims=True))
    target = lax.broadcasted_iota(jnp.int32, (1, LANES), 1) * group_size + group_size // 2
    target = jnp.where((target > group_size) & (target < group_size * group_size), target, -1).astype(f32)
    found = jnp.zeros((tiles, LANES), f32)
    for i in range(group_size):
        for a in samples(i):
            less = jnp.zeros((tiles, LANES), f32)
            for b in packed:
                less += (b < a).astype(f32)
            rank = jnp.sum(less, axis=1, keepdims=True)
            found += jnp.where(rank == target, a, 0.0)
    splitters = jnp.sum(found, axis=0, keepdims=True)
    splitters = jnp.sum(jnp.where(group_lane == group_sub, splitters, 0.0), axis=1, keepdims=True)
    splitters = jnp.where(group_sub == 0, -PAD_KEY, splitters)

    edge_ref[...] = jnp.zeros(edge_ref.shape, f32)

    def count(b, carry):
        edges = edge_ref[...]
        for u in range(4):
            i = b * 4 + u
            less = jnp.zeros((group_size, LANES), f32)
            for r in range(tiles):
                less += (all_ref[i, r : r + 1, :] < splitters).astype(f32)
            edges = jnp.where(group_lane == i, jnp.sum(less, axis=1, keepdims=True), edges)
        edge_ref[...] = edges
        return carry

    lax.fori_loop(0, group_size // 4, count, 0)
    edges = edge_ref[...]
    after = jnp.concatenate([edges[1:], jnp.full((1, LANES), n_dev, f32)], 0)
    counts = jnp.where(group_lane < group_size, after - edges, 0.0)
    over = jnp.maximum(counts - cap, 0.0)
    has = (over > 0).astype(f32)
    worst = jnp.maximum(jnp.max(jnp.sum(has, axis=0, keepdims=True), axis=1, keepdims=True), jnp.max(jnp.sum(has, axis=1, keepdims=True), axis=0, keepdims=True))
    most_over = jnp.max(jnp.max(over, axis=0, keepdims=True), axis=1, keepdims=True)
    short = ((worst <= 1) & (most_over <= most)).astype(f32)

    def to_row(column):
        return jnp.sum(jnp.where(group_lane == group_sub, column, 0.0), axis=0, keepdims=True)

    mine = group_lane == me
    starts = to_row(jnp.sum(jnp.where(mine, edges, 0.0), axis=1, keepdims=True))
    col_starts = jnp.sum(jnp.where(group_sub == me, edges, 0.0), axis=0, keepdims=True)
    col_counts = jnp.sum(jnp.where(group_sub == me, counts, 0.0), axis=0, keepdims=True)
    from_src = to_row(jnp.sum(has * group_lane.astype(f32), axis=1, keepdims=True))
    extra = jnp.sum(jnp.sum(jnp.where(mine, has * (edges + cap), 0.0), axis=0, keepdims=True), axis=1, keepdims=True)
    own = jnp.sum(col_counts, axis=1, keepdims=True)
    rows = [starts, col_starts, col_counts, from_src, extra, short, own, own]
    return jnp.concatenate([jnp.broadcast_to(r, (1, LANES)) for r in rows], 0).astype(jnp.int32)


def take_segments(cap, relay, table_ref, all_ref, out_ref, slot_ref):
    group_size, tiles, _ = all_ref.shape
    lane = lax.broadcasted_iota(jnp.int32, (1, LANES), 1)
    short = table_ref[SHORT, 0] > 0
    past = lane - cap
    relayed = group_size * cap + lax.rem(past, group_size) * relay + past // group_size
    unused = jnp.where(short, group_size * (cap + relay), group_size * LANES)
    for i in range(group_size):
        s = jnp.clip(table_ref[COL_STARTS, i], 0, tiles * LANES - 1)
        t = s // LANES
        off = s - t * LANES
        a = all_ref[i, pl.ds(t, 1), :]
        b = all_ref[i, pl.ds(jnp.minimum(t + 1, tiles - 1), 1), :]
        shift = lax.rem(LANES - off, LANES)
        a = pltpu.roll(a, shift, 1)
        b = pltpu.roll(b, shift, 1)
        v = jnp.where(lane < LANES - off, a, b)
        live = lane < table_ref[COL_COUNTS, i]
        out_ref[pl.ds(i, 1), :] = jnp.where(live, v, PAD_KEY)
        slot = jnp.where(short, jnp.where(past < 0, i * cap + lane, relayed), i * LANES + lane)
        slot_ref[pl.ds(i, 1), :] = jnp.where(live, slot, unused)


def sort_exchange_kernel(
    group_size, cap, relay, block,
    keys_ref, rows_ref,
    out_ref, merged_ref, idx_ref, order_ref, split_ref, table_ref,
    fetched, held, outgoing, first, arrived, second, mine, all_ref, edge_ref, seg_ref, slot_ref, order, table,
    in_sem, own_sem, send_sem, recv_sem,
):
    me = lax.axis_index("g")
    core, x, y = lax.rem(me, CORES), lax.rem(me // CORES, SIDE), me // (CORES * SIDE)
    n, width = rows_ref.shape
    tiles = width // LANES

    def peer(d):
        return lax.rem(me + d, group_size)

    barrier = pltpu.get_barrier_semaphore()
    for d in range(1, group_size):
        pl.semaphore_signal(barrier, inc=1, device_id={"g": peer(d)}, device_id_type=MESH)

    def fetch(s):
        return pltpu.make_async_copy(rows_ref.at[pl.ds(s * block, block)], fetched.at[s], in_sem.at[s])

    def split(s):
        fetch(s).wait()

        def body(g, carry):
            r = pl.multiple_of(g * 16, 16)
            v = fetched[s, pl.ds(r, 16), :].reshape(16, tiles, LANES)
            for q in range(tiles // SUB):
                held[pl.ds(s * block + r, 16), q] = v[:, SUB * q : SUB * (q + 1)]
            return carry

        lax.fori_loop(0, block // 16, body, 0)

    for s in range(n // block):
        fetch(s).start()
    shape = keys_ref.shape
    places = lax.broadcasted_iota(jnp.int32, shape, 0) * LANES + lax.broadcasted_iota(jnp.int32, shape, 1)
    sorted_keys, sorted_places = bitonic_sort(keys_ref[...], places)
    mine[...] = sorted_keys
    order_ref[...] = sorted_places
    all_ref[pl.ds(me, 1)] = sorted_keys[None]
    split(0)
    pl.semaphore_wait(barrier, group_size - 1)

    def remote(d, dst, src_ref, dst_ref, kind):
        return pltpu.make_async_remote_copy(
            src_ref=src_ref, dst_ref=dst_ref, send_sem=send_sem.at[kind, d], recv_sem=recv_sem.at[kind, d], device_id={"g": dst}, device_id_type=MESH
        )

    def share(d):
        return remote(d, peer(d), mine, all_ref.at[me], 3)

    def hop_one(d):
        return remote(d, peer(d), first.at[peer(d)], arrived.at[me], 1)

    def hop_two(d):
        return remote(d, peer(d), second.at[peer(d)], out_ref.at[pl.ds(group_size * cap + me * relay, relay)], 2)

    def far(s):
        dx, dy, dc = STEPS[s]
        return (lax.rem(y + dy, SIDE) * SIDE + lax.rem(x + dx, SIDE)) * CORES + lax.rem(core + dc, CORES)

    def base(s):
        return remote(s, far(s), outgoing.at[far(s)], out_ref.at[pl.ds(me * cap, cap)], 0)

    def each(act):
        def body(d, carry):
            act(d)
            return carry

        lax.fori_loop(1, group_size, body, 0)

    each(lambda d: share(d).start())
    for s in range(1, n // block):
        split(s)
    to_order = pltpu.make_async_copy(order_ref, order, own_sem.at[2])
    to_order.start()
    each(lambda d: share(d).wait())
    table_ref[...] = make_plan(me, cap, relay * group_size, all_ref, edge_ref)
    to_table = pltpu.make_async_copy(table_ref, table, own_sem.at[3])
    to_table.start()
    to_order.wait()
    to_table.wait()

    last = n - 1

    def row(k):
        k = jnp.minimum(k, last)
        return held[jnp.clip(order[k // LANES, lax.rem(k, LANES)], 0, last)]

    def gather(dst):
        begin = jnp.clip(table[STARTS, dst], 0, last)

        def body(b, carry):
            for u in range(5):
                k = b * 5 + u
                outgoing[dst, k] = row(begin + k)
            return carry

        lax.fori_loop(0, cap // 5, body, 0)

    extra = jnp.clip(table[EXTRA, 0], 0, last)

    def gather_extra(m, carry):
        for r in range(relay):
            first[m, r] = row(extra + r * group_size + m)
        return carry

    lax.fori_loop(0, group_size, gather_extra, 0)
    arrived[pl.ds(me, 1)] = first[pl.ds(me, 1)]
    gather(far(0))
    each(lambda d: hop_one(d).start())
    for s in range(group_size - 1):
        if s >= WINDOW:
            base(s - WINDOW).wait_send()
        if s + 1 < group_size - 1:
            gather(far(s + 1))
        base(s).start()
        if s == WINDOW:
            each(lambda d: hop_one(d).wait())
            for j in range(group_size):
                second[j] = arrived[jnp.clip(table[FROM_SRC, j], 0, group_size - 1)]
            gather(me)
        if s == WINDOW + 1:
            each(lambda d: hop_two(d).start())
            own_two = pltpu.make_async_copy(second.at[me], out_ref.at[pl.ds(group_size * cap + me * relay, relay)], own_sem.at[1])
            own_base = pltpu.make_async_copy(outgoing.at[me], out_ref.at[pl.ds(me * cap, cap)], own_sem.at[0])
            own_two.start()
            own_base.start()
        if s == WINDOW + 4:
            take_segments(cap, relay, table, all_ref, seg_ref, slot_ref)
            merged_ref[...], idx_ref[...] = bitonic_sort(seg_ref[...], slot_ref[...])
    keep = pltpu.make_async_copy(held, split_ref, own_sem.at[4])
    keep.start()
    for s in range(group_size - 1):
        if s >= group_size - 1 - WINDOW:
            base(s).wait_send()
        base(s).wait_recv()
    each(lambda d: hop_two(d).wait())
    own_two.wait()
    own_base.wait()
    keep.wait()


def sort_exchange(keys, rows, cap, relay, group_size):
    n, width = rows.shape
    block = 512
    row = (width // (SUB * LANES), SUB, LANES)
    segs = (group_size, LANES)
    sems = pltpu.SemaphoreType.DMA
    return pl.pallas_call(
        functools.partial(sort_exchange_kernel, group_size, cap, relay, block),
        out_shape=[
            jax.ShapeDtypeStruct((group_size * (cap + relay), *row), rows.dtype),
            jax.ShapeDtypeStruct(segs, keys.dtype),
            jax.ShapeDtypeStruct(segs, jnp.int32),
            jax.ShapeDtypeStruct(keys.shape, jnp.int32),
            jax.ShapeDtypeStruct((n, *row), rows.dtype),
            jax.ShapeDtypeStruct((8, LANES), jnp.int32),
        ],
        in_specs=[VMEM, ANY],
        out_specs=[ANY, VMEM, VMEM, VMEM, ANY, VMEM],
        scratch_shapes=[
            pltpu.VMEM((n // block, block, width), rows.dtype),
            pltpu.VMEM((n, *row), rows.dtype),
            pltpu.VMEM((group_size, cap, *row), rows.dtype),
            pltpu.VMEM((group_size, relay, *row), rows.dtype),
            pltpu.VMEM((group_size, relay, *row), rows.dtype),
            pltpu.VMEM((group_size, relay, *row), rows.dtype),
            pltpu.VMEM(keys.shape, keys.dtype),
            pltpu.VMEM((group_size, *keys.shape), keys.dtype),
            pltpu.VMEM(segs, jnp.float32),
            pltpu.VMEM(segs, keys.dtype),
            pltpu.VMEM(segs, jnp.int32),
            pltpu.SMEM(keys.shape, jnp.int32),
            pltpu.SMEM((8, LANES), jnp.int32),
            sems((n // block,)),
            sems((5,)),
            sems((4, group_size)),
            sems((4, group_size)),
        ],
        compiler_params=pltpu.CompilerParams(collective_id=0, has_side_effects=True),
        name="sort_exchange",
    )(keys, rows)


def pick_kernel(cap, group_size, order_ref, table_ref, rows_ref, out_ref):
    last = rows_ref.shape[0] - 1

    def per_dst(j, carry):
        first = table_ref[STARTS, j]

        def body(b, c):
            for u in range(8):
                k = b * 8 + u
                out_ref[j, k] = rows_ref[order_ref[jnp.minimum(first + k, last)]]
            return c

        return lax.fori_loop(0, cap // 8, body, carry)

    lax.fori_loop(0, group_size, per_dst, 0)


def pick(order, table, rows, cap, group_size):
    return pl.pallas_call(
        functools.partial(pick_kernel, cap, group_size),
        out_shape=jax.ShapeDtypeStruct((group_size, cap, *rows.shape[1:]), rows.dtype),
        in_specs=[SMEM, SMEM, VMEM],
        out_specs=VMEM,
        name="pick_rows",
    )(order, table, rows)


def place_kernel(idx_ref, count_ref, in_ref, out_ref, held, staged, blank, in_sem, out_sem, blank_sem):
    slots, block, width = staged.shape
    total = in_ref.shape[0]
    parts = held.shape[1]
    load = pltpu.make_async_copy(in_ref, held.at[pl.ds(0, total)], in_sem)
    load.start()
    blank[...] = jnp.zeros(blank.shape, blank.dtype)
    held[total] = jnp.zeros(held.shape[1:], held.dtype)
    steps = out_ref.shape[0] // block
    live = pl.cdiv(count_ref[0], block)

    def clear(s):
        return pltpu.make_async_copy(blank, out_ref.at[pl.ds(s * block, block)], blank_sem)

    def store(s):
        slot = lax.rem(s, slots)
        return pltpu.make_async_copy(staged.at[slot], out_ref.at[pl.ds(s * block, block)], out_sem.at[slot])

    load.wait()

    def start_clear(s, carry):
        clear(s).start()
        return carry

    lax.fori_loop(live, steps, start_clear, 0)

    def step(s, carry):
        @pl.when(s >= slots)
        def _():
            store(s - slots).wait()

        slot = lax.rem(s, slots)

        def body(g, c):
            r = pl.multiple_of(g * 16, 16)
            rows = []
            for u in range(16):
                k = idx_ref[s * block + r + u]
                rows.append(jnp.concatenate([held[k, q] for q in range(parts)], 0))
            staged[slot, pl.ds(r, 16), :] = jnp.stack(rows, 0).reshape(16, width)
            return c

        lax.fori_loop(0, block // 16, body, 0)
        store(s).start()
        return carry

    lax.fori_loop(0, live, step, 0)

    def end_store(s, carry):
        store(s).wait()
        return carry

    lax.fori_loop(jnp.maximum(live - slots, 0), live, end_store, 0)

    def end_clear(s, carry):
        clear(s).wait()
        return carry

    lax.fori_loop(live, steps, end_clear, 0)


def place(idx, count, rows, width):
    n_out = idx.shape[0]
    block, slots = 128, 4
    return pl.pallas_call(
        place_kernel,
        out_shape=jax.ShapeDtypeStruct((n_out, width), rows.dtype),
        in_specs=[SMEM, SMEM, ANY],
        out_specs=ANY,
        scratch_shapes=[
            pltpu.VMEM((rows.shape[0] + 1, *rows.shape[1:]), rows.dtype),
            pltpu.VMEM((slots, block, width), rows.dtype),
            pltpu.VMEM((block, width), rows.dtype),
            pltpu.SemaphoreType.DMA,
            pltpu.SemaphoreType.DMA((slots,)),
            pltpu.SemaphoreType.DMA,
        ],
        name="place_rows",
    )(idx, count, rows)


def solution(mesh):
    group_size = mesh.shape["g"]

    def local_part(keys_loc, rows_loc):
        n_dev = keys_loc.shape[0]
        width = rows_loc.shape[1]
        cap_rows = 2 * n_dev // group_size
        blocks, merged, idx, order, rows, table = sort_exchange(keys_loc.reshape(n_dev // LANES, LANES), rows_loc, BASE, RELAY, group_size)
        own_count = table[OWN, :1]
        idx = idx.reshape(-1)

        def arrived():
            return place(idx, own_count, blocks, width)

        def direct():
            wide = lax.all_to_all(pick(order.reshape(-1), table, rows, cap_rows, group_size), "g", 0, 0, tiled=True)
            return place(idx, own_count, wide.reshape(-1, *wide.shape[2:]), width)

        merged_rows = lax.cond(table[SHORT, 0] > 0, arrived, direct)
        return merged.reshape(-1), merged_rows, own_count

    row_spec = P(("batch", "g"))
    mat_spec = P(("batch", "g"), None)
    return jax.shard_map(local_part, mesh=mesh, in_specs=(row_spec, mat_spec), out_specs=(row_spec, mat_spec, row_spec), check_vma=False)
```

time: 179 us -> 119 us (0.66)
  Pallas kernels: 163 us -> 116 us
  other arithmetic: 12.9 us -> 0 us
    pallas_call x4 -> x1, Pallas kernels: 152 us -> 104 us  [sort_exchange(): pl.pallas_call(functools.partial(sort_exchange_kernel, group_size, cap, r...]
    sort x2 -> x0, other arithmetic: 12.9 us -> none  [the longest x1 7.01 us: local_part(): merged, idx = lax.sort((segs.reshape(-1), slots.reshape(-1)), num_keys=1)]
where the time goes in v3:
time: 119 us
  Pallas kernels  116 us (97%)
  between operations  1.32 us (1%)
    pallas_call x1, Pallas kernels, sort_exchange(): pl.pallas_call(functools.partial(sort_exchange_kernel, group_size, cap, r...  104 us
    pallas_call x1, Pallas kernels, place(): pl.pallas_call(place_kernel, out_shape=jax.ShapeDtypeStruct((n_out, width...  11.8 us

profile of v3, /device:TPU:97, one launch (start us, length us, event | category | flops | bytes accessed | tf_op | source)
XLA Modules:
  0.0 118.7 jit_solution(14171920014421434791)
XLA Ops:
  0.6 104.4 %sort_exchange.1 = (bf16[2144,3,4,128]{3,2,1,0:T(4,128)(2,1)}, f32[32,128]{1,0:T(8,128)}, s32[32,128]{1,0:T(8,128)S(1)}, s32[16,128]{1,0:T(8,128)S(1)}, bf16[204...) custom-call(f32[16,128]{1,0:T(8,128)} %bitcast.11, bf16[2048,1536]{1,0:T(8,128)(2,1)} %rows_ref.1), custom_call_target="tpu_custom_call" | custom-call | tf_op jit(solution)/shard_map/sort_exchange/pallas_call | solution.py:298
  105.1 0.5 fusion
  106.2 0.0 copy-start
  106.2 11.8 %conditional.1 = (bf16[4096,1536]{1,0:T(8,128)(2,1)}) conditional(s32[]{:T(128)} %bitcast.4, (s32[16,128]{1,0:T(8,128)S(1)}, s32[8,128]{1,0:T(8,128)S(1)}, bf16[2048,3,4,128]{3,2,1,0:T(4,128)(2,1)}, s32[4096]{0:T(1024)S(1)}, s32[1]{0:T(128)}) %tuple.22, (s32[4096]{0:T(1024)S(1)}, s32[1]{0:T(128)}, bf16[2144,3,4,128]{3,2,1,0:T(4,128)(2,1)}) %tuple.23), branch_computations={%region_0.0_spmd, %region_1.0_spmd} | conditional | bytes 25165832 | solution.py:460
  106.3 11.8 %place_rows.3 = bf16[4096,1536]{1,0:T(8,128)(2,1)} custom-call(s32[4096]{0:T(1024)S(1)} %get-tuple-element.24.idx_ref, s32[1]{0:T(128)} %get-tuple-element.25.count_ref, bf16[2144,3,4,128]{3,2,1,0:T(4,128)(2,1)} %get-tuple-element.26.in_ref), custom_call_target="tpu_custom_call" | custom-call | tf_op jit(solution)/shard_map/cond/branch_1_fun/place_rows/pallas_call | solution.py:425
  118.0 0.0 copy-done
  118.0 0.6 copy.8
Async XLA Ops:
  106.2 11.8 %copy-start = (f32[32,128]{1,0:T(8,128)S(1)}, f32[32,128]{1,0:T(8,128)}, u32[]{:S(2)}) copy-start(f32[32,128]{1,0:T(8,128)} %get-tuple-element.36) | copy-start | bytes 49156

commit v4 on v3

--- a/solution.py
+++ b/solution.py
@@ -48,77 +48,90 @@
     return keys, vals
 
 
-def make_plan(me, cap, most, all_ref, edge_ref):
+def sample_row(keys, group_size):
+    rows, lanes = keys.shape
+    per = rows * lanes // group_size
+    each = lanes // per
+    lane = lax.broadcasted_iota(jnp.int32, keys.shape, 1)
+    sub = lax.broadcasted_iota(jnp.int32, keys.shape, 0)
+    acc = jnp.zeros(keys.shape, keys.dtype)
+    for l in range(each):
+        acc = jnp.where(lane == each * sub + l, keys[:, l * per : l * per + 1], acc)
+    return jnp.sum(acc, axis=0, keepdims=True)
+
+
+def pick_splitters(samples):
+    group_size = samples.shape[0]
+    lane = lax.broadcasted_iota(jnp.int32, samples.shape, 1)
+    sub = lax.broadcasted_iota(jnp.int32, samples.shape, 0)
+    fit = LANES // group_size
+    merged = samples
+    for f in range(1, fit):
+        merged = jnp.where(lax.rem(sub, fit) == f, pltpu.roll(samples, f * group_size, 1), merged)
+    packed = [jnp.sum(merged[c * fit : (c + 1) * fit], axis=0, keepdims=True) for c in range(group_size // fit)]
+    less = [jnp.zeros(samples.shape, jnp.float32) for _ in packed]
+    for q in range(group_size):
+        a = jnp.broadcast_to(samples[:, q : q + 1], samples.shape)
+        less = [n + (a < b).astype(jnp.float32) for n, b in zip(less, packed)]
+    target = (sub * group_size + group_size // 2).astype(jnp.float32)
+    found = jnp.zeros(samples.shape, jnp.float32)
+    for n, b in zip(less, packed):
+        found += jnp.where(jnp.sum(n, axis=0, keepdims=True) == target, b, 0.0)
+    return jnp.where(sub == 0, -PAD_KEY, jnp.sum(found, axis=1, keepdims=True))
+
+
+def count_below(keys, splitters):
+    less = jnp.zeros(splitters.shape, jnp.float32)
+    for r in range(keys.shape[0]):
+        less += (keys[r : r + 1] < splitters).astype(jnp.float32)
+    return jnp.sum(less, axis=1, keepdims=True)
+
+
+def to_row(column, shape):
+    lane = lax.broadcasted_iota(jnp.int32, shape, 1)
+    sub = lax.broadcasted_iota(jnp.int32, shape, 0)
+    return jnp.sum(jnp.where(lane == sub, column, 0.0), axis=0, keepdims=True)
+
+
+def to_table(rows):
+    rows = rows + [rows[-1]] * (8 - len(rows))
+    return jnp.concatenate([jnp.broadcast_to(r, (1, LANES)) for r in rows], 0).astype(jnp.int32)
+
+
+def make_plan(me, cap, most, all_ref, split_ref, edge_ref):
     group_size, tiles, _ = all_ref.shape
     n_dev = tiles * LANES
-    per = n_dev // group_size
-    each = LANES // per
-    f32 = jnp.float32
-    lane = lax.broadcasted_iota(jnp.int32, (tiles, LANES), 1)
-    sub = lax.broadcasted_iota(jnp.int32, (tiles, LANES), 0)
-    group_lane = lax.broadcasted_iota(jnp.int32, (group_size, LANES), 1)
-    group_sub = lax.broadcasted_iota(jnp.int32, (group_size, LANES), 0)
-
-    def samples(i):
-        return [jnp.broadcast_to(all_ref[i, :, l * per : l * per + 1], (tiles, LANES)) for l in range(each)]
-
-    fit = LANES // group_size
-    packed = []
-    for c in range(group_size // fit):
-        acc = jnp.zeros((tiles, LANES), f32)
-        for i in range(c * fit, (c + 1) * fit):
-            for l, a in enumerate(samples(i)):
-                acc = jnp.where(lane == (i % fit) * group_size + each * sub + l, a, acc)
-        packed.append(jnp.sum(acc, axis=0, keepdims=True))
-    target = lax.broadcasted_iota(jnp.int32, (1, LANES), 1) * group_size + group_size // 2
-    target = jnp.where((target > group_size) & (target < group_size * group_size), target, -1).astype(f32)
-    found = jnp.zeros((tiles, LANES), f32)
-    for i in range(group_size):
-        for a in samples(i):
-            less = jnp.zeros((tiles, LANES), f32)
-            for b in packed:
-                less += (b < a).astype(f32)
-            rank = jnp.sum(less, axis=1, keepdims=True)
-            found += jnp.where(rank == target, a, 0.0)
-    splitters = jnp.sum(found, axis=0, keepdims=True)
-    splitters = jnp.sum(jnp.where(group_lane == group_sub, splitters, 0.0), axis=1, keepdims=True)
-    splitters = jnp.where(group_sub == 0, -PAD_KEY, splitters)
-
-    edge_ref[...] = jnp.zeros(edge_ref.shape, f32)
+    shape = edge_ref.shape
+    lane = lax.broadcasted_iota(jnp.int32, shape, 1)
+    sub = lax.broadcasted_iota(jnp.int32, shape, 0)
+    splitters = split_ref[...]
+    edge_ref[...] = jnp.zeros(shape, jnp.float32)
 
     def count(b, carry):
         edges = edge_ref[...]
         for u in range(4):
             i = b * 4 + u
-            less = jnp.zeros((group_size, LANES), f32)
-            for r in range(tiles):
-                less += (all_ref[i, r : r + 1, :] < splitters).astype(f32)
-            edges = jnp.where(group_lane == i, jnp.sum(less, axis=1, keepdims=True), edges)
+            edges = jnp.where(lane == i, count_below(all_ref[i], splitters), edges)
         edge_ref[...] = edges
         return carry
 
     lax.fori_loop(0, group_size // 4, count, 0)
     edges = edge_ref[...]
-    after = jnp.concatenate([edges[1:], jnp.full((1, LANES), n_dev, f32)], 0)
-    counts = jnp.where(group_lane < group_size, after - edges, 0.0)
+    after = jnp.concatenate([edges[1:], jnp.full((1, LANES), n_dev, jnp.float32)], 0)
+    counts = jnp.where(lane < group_size, after - edges, 0.0)
     over = jnp.maximum(counts - cap, 0.0)
-    has = (over > 0).astype(f32)
+    has = (over > 0).astype(jnp.float32)
     worst = jnp.maximum(jnp.max(jnp.sum(has, axis=0, keepdims=True), axis=1, keepdims=True), jnp.max(jnp.sum(has, axis=1, keepdims=True), axis=0, keepdims=True))
     most_over = jnp.max(jnp.max(over, axis=0, keepdims=True), axis=1, keepdims=True)
-    short = ((worst <= 1) & (most_over <= most)).astype(f32)
-
-    def to_row(column):
-        return jnp.sum(jnp.where(group_lane == group_sub, column, 0.0), axis=0, keepdims=True)
-
-    mine = group_lane == me
-    starts = to_row(jnp.sum(jnp.where(mine, edges, 0.0), axis=1, keepdims=True))
-    col_starts = jnp.sum(jnp.where(group_sub == me, edges, 0.0), axis=0, keepdims=True)
-    col_counts = jnp.sum(jnp.where(group_sub == me, counts, 0.0), axis=0, keepdims=True)
-    from_src = to_row(jnp.sum(has * group_lane.astype(f32), axis=1, keepdims=True))
+    short = ((worst <= 1) & (most_over <= most)).astype(jnp.float32)
+    mine = lane == me
+    starts = to_row(jnp.sum(jnp.where(mine, edges, 0.0), axis=1, keepdims=True), shape)
+    col_starts = jnp.sum(jnp.where(sub == me, edges, 0.0), axis=0, keepdims=True)
+    col_counts = jnp.sum(jnp.where(sub == me, counts, 0.0), axis=0, keepdims=True)
+    from_src = to_row(jnp.sum(has * lane.astype(jnp.float32), axis=1, keepdims=True), shape)
     extra = jnp.sum(jnp.sum(jnp.where(mine, has * (edges + cap), 0.0), axis=0, keepdims=True), axis=1, keepdims=True)
     own = jnp.sum(col_counts, axis=1, keepdims=True)
-    rows = [starts, col_starts, col_counts, from_src, extra, short, own, own]
-    return jnp.concatenate([jnp.broadcast_to(r, (1, LANES)) for r in rows], 0).astype(jnp.int32)
+    return to_table([starts, col_starts, col_counts, from_src, extra, short, own])
 
 
 def take_segments(cap, relay, table_ref, all_ref, out_ref, slot_ref):
@@ -147,8 +160,8 @@
 def sort_exchange_kernel(
     group_size, cap, relay, block,
     keys_ref, rows_ref,
-    out_ref, merged_ref, idx_ref, order_ref, split_ref, table_ref,
-    fetched, held, outgoing, first, arrived, second, mine, all_ref, edge_ref, seg_ref, slot_ref, order, table,
+    out_ref, merged_ref, idx_ref, order_ref, split_ref, table_ref, own_ref, short_ref,
+    fetched, held, outgoing, first, arrived, second, mine, all_ref, my_samples, samples, start_ref, splitters, edge_ref, seg_ref, slot_ref, order, starts, table,
     in_sem, own_sem, send_sem, recv_sem,
 ):
     me = lax.axis_index("g")
@@ -186,6 +199,8 @@
     mine[...] = sorted_keys
     order_ref[...] = sorted_places
     all_ref[pl.ds(me, 1)] = sorted_keys[None]
+    my_samples[...] = sample_row(sorted_keys, group_size)
+    samples[pl.ds(me, 1)] = my_samples[...][None]
     split(0)
     pl.semaphore_wait(barrier, group_size - 1)
 
@@ -197,6 +212,9 @@
     def share(d):
         return remote(d, peer(d), mine, all_ref.at[me], 3)
 
+    def share_samples(d):
+        return remote(d, peer(d), my_samples, samples.at[me], 4)
+
     def hop_one(d):
         return remote(d, peer(d), first.at[peer(d)], arrived.at[me], 1)
 
@@ -217,46 +235,40 @@
 
         lax.fori_loop(1, group_size, body, 0)
 
+    each(lambda d: share_samples(d).start())
     each(lambda d: share(d).start())
+    to_order = pltpu.make_async_copy(order_ref, order, own_sem.at[2])
+    to_order.start()
     for s in range(1, n // block):
         split(s)
-    to_order = pltpu.make_async_copy(order_ref, order, own_sem.at[2])
-    to_order.start()
-    each(lambda d: share(d).wait())
-    table_ref[...] = make_plan(me, cap, relay * group_size, all_ref, edge_ref)
-    to_table = pltpu.make_async_copy(table_ref, table, own_sem.at[3])
-    to_table.start()
+    each(lambda d: share_samples(d).wait())
+    splitters[...] = pick_splitters(samples[:, 0, :])
+    start_ref[...] = to_table([to_row(count_below(mine[...], splitters[...]), edge_ref.shape)])
+    to_starts = pltpu.make_async_copy(start_ref, starts, own_sem.at[3])
+    to_starts.start()
     to_order.wait()
-    to_table.wait()
+    to_starts.wait()
 
     last = n - 1
 
     def row(k):
-        k = jnp.minimum(k, last)
-        return held[jnp.clip(order[k // LANES, lax.rem(k, LANES)], 0, last)]
+        k = k & last
+        return held[order[k >> 7, k & (LANES - 1)] & last]
 
     def gather(dst):
-        begin = jnp.clip(table[STARTS, dst], 0, last)
+        begin = starts[STARTS, dst]
 
         def body(b, carry):
-            for u in range(5):
-                k = b * 5 + u
+            for u in range(13):
+                k = b * 13 + u
                 outgoing[dst, k] = row(begin + k)
             return carry
 
-        lax.fori_loop(0, cap // 5, body, 0)
-
-    extra = jnp.clip(table[EXTRA, 0], 0, last)
-
-    def gather_extra(m, carry):
-        for r in range(relay):
-            first[m, r] = row(extra + r * group_size + m)
-        return carry
-
-    lax.fori_loop(0, group_size, gather_extra, 0)
-    arrived[pl.ds(me, 1)] = first[pl.ds(me, 1)]
+        lax.fori_loop(0, cap // 13, body, 0)
+
+    own_two = pltpu.make_async_copy(second.at[me], out_ref.at[pl.ds(group_size * cap + me * relay, relay)], own_sem.at[1])
+    own_base = pltpu.make_async_copy(outgoing.at[me], out_ref.at[pl.ds(me * cap, cap)], own_sem.at[0])
     gather(far(0))
-    each(lambda d: hop_one(d).start())
     for s in range(group_size - 1):
         if s >= WINDOW:
             base(s - WINDOW).wait_send()
@@ -264,19 +276,39 @@
             gather(far(s + 1))
         base(s).start()
         if s == WINDOW:
+            each(lambda d: share(d).wait())
+            table_ref[...] = make_plan(me, cap, relay * group_size, all_ref, splitters, edge_ref)
+            to_smem = pltpu.make_async_copy(table_ref, table, own_sem.at[5])
+            to_smem.start()
+            gather(me)
+            to_smem.wait()
+        if s == WINDOW + 1:
+            extra = table[EXTRA, 0]
+
+            def gather_extra(b, carry):
+                for u in range(8):
+                    m = b * 8 + u
+                    for r in range(relay):
+                        first[m, r] = row(extra + r * group_size + m)
+                return carry
+
+            lax.fori_loop(0, group_size // 8, gather_extra, 0)
+            arrived[pl.ds(me, 1)] = first[pl.ds(me, 1)]
+            own_base.start()
+        if s == WINDOW + 2:
+            each(lambda d: hop_one(d).start())
+        if s == WINDOW + 4:
+            own_ref[0] = table[OWN, 0]
+            short_ref[0] = table[SHORT, 0]
+            take_segments(cap, relay, table, all_ref, seg_ref, slot_ref)
+            merged_ref[...], idx_ref[...] = bitonic_sort(seg_ref[...], slot_ref[...])
+        if s == WINDOW + 12:
             each(lambda d: hop_one(d).wait())
             for j in range(group_size):
-                second[j] = arrived[jnp.clip(table[FROM_SRC, j], 0, group_size - 1)]
-            gather(me)
-        if s == WINDOW + 1:
+                second[j] = arrived[table[FROM_SRC, j] & (group_size - 1)]
+        if s == WINDOW + 13:
             each(lambda d: hop_two(d).start())
-            own_two = pltpu.make_async_copy(second.at[me], out_ref.at[pl.ds(group_size * cap + me * relay, relay)], own_sem.at[1])
-            own_base = pltpu.make_async_copy(outgoing.at[me], out_ref.at[pl.ds(me * cap, cap)], own_sem.at[0])
             own_two.start()
-            own_base.start()
-        if s == WINDOW + 4:
-            take_segments(cap, relay, table, all_ref, seg_ref, slot_ref)
-            merged_ref[...], idx_ref[...] = bitonic_sort(seg_ref[...], slot_ref[...])
     keep = pltpu.make_async_copy(held, split_ref, own_sem.at[4])
     keep.start()
     for s in range(group_size - 1):
@@ -304,9 +336,11 @@
             jax.ShapeDtypeStruct(keys.shape, jnp.int32),
             jax.ShapeDtypeStruct((n, *row), rows.dtype),
             jax.ShapeDtypeStruct((8, LANES), jnp.int32),
+            jax.ShapeDtypeStruct((1,), jnp.int32),
+            jax.ShapeDtypeStruct((1,), jnp.int32),
         ],
         in_specs=[VMEM, ANY],
-        out_specs=[ANY, VMEM, VMEM, VMEM, ANY, VMEM],
+        out_specs=[ANY, VMEM, VMEM, VMEM, ANY, VMEM, SMEM, SMEM],
         scratch_shapes=[
             pltpu.VMEM((n // block, block, width), rows.dtype),
             pltpu.VMEM((n, *row), rows.dtype),
@@ -316,15 +350,20 @@
             pltpu.VMEM((group_size, relay, *row), rows.dtype),
             pltpu.VMEM(keys.shape, keys.dtype),
             pltpu.VMEM((group_size, *keys.shape), keys.dtype),
+            pltpu.VMEM((1, LANES), keys.dtype),
+            pltpu.VMEM((group_size, 1, LANES), keys.dtype),
+            pltpu.VMEM((8, LANES), jnp.int32),
+            pltpu.VMEM(segs, keys.dtype),
             pltpu.VMEM(segs, jnp.float32),
             pltpu.VMEM(segs, keys.dtype),
             pltpu.VMEM(segs, jnp.int32),
             pltpu.SMEM(keys.shape, jnp.int32),
             pltpu.SMEM((8, LANES), jnp.int32),
+            pltpu.SMEM((8, LANES), jnp.int32),
             sems((n // block,)),
-            sems((5,)),
-            sems((4, group_size)),
-            sems((4, group_size)),
+            sems((6,)),
+            sems((5, group_size)),
+            sems((5, group_size)),
         ],
         compiler_params=pltpu.CompilerParams(collective_id=0, has_side_effects=True),
         name="sort_exchange",
@@ -358,12 +397,13 @@
     )(order, table, rows)
 
 
-def place_kernel(idx_ref, count_ref, in_ref, out_ref, held, staged, blank, in_sem, out_sem, blank_sem):
+def place_kernel(idx_ref, count_ref, in_ref, keys_ref, out_ref, out_keys_ref, held, staged, blank, in_sem, out_sem, blank_sem):
     slots, block, width = staged.shape
     total = in_ref.shape[0]
     parts = held.shape[1]
     load = pltpu.make_async_copy(in_ref, held.at[pl.ds(0, total)], in_sem)
     load.start()
+    out_keys_ref[...] = keys_ref[...]
     blank[...] = jnp.zeros(blank.shape, blank.dtype)
     held[total] = jnp.zeros(held.shape[1:], held.dtype)
     steps = out_ref.shape[0] // block
@@ -419,14 +459,14 @@
     lax.fori_loop(live, steps, end_clear, 0)
 
 
-def place(idx, count, rows, width):
+def place(idx, count, rows, keys, width):
     n_out = idx.shape[0]
     block, slots = 128, 4
     return pl.pallas_call(
         place_kernel,
-        out_shape=jax.ShapeDtypeStruct((n_out, width), rows.dtype),
-        in_specs=[SMEM, SMEM, ANY],
-        out_specs=ANY,
+        out_shape=[jax.ShapeDtypeStruct((n_out, width), rows.dtype), jax.ShapeDtypeStruct(keys.shape, keys.dtype)],
+        in_specs=[SMEM, SMEM, ANY, VMEM],
+        out_specs=[ANY, VMEM],
         scratch_shapes=[
             pltpu.VMEM((rows.shape[0] + 1, *rows.shape[1:]), rows.dtype),
             pltpu.VMEM((slots, block, width), rows.dtype),
@@ -436,7 +476,7 @@
             pltpu.SemaphoreType.DMA,
         ],
         name="place_rows",
-    )(idx, count, rows)
+    )(idx, count, rows, keys)
 
 
 def solution(mesh):
@@ -446,19 +486,18 @@
         n_dev = keys_loc.shape[0]
         width = rows_loc.shape[1]
         cap_rows = 2 * n_dev // group_size
-        blocks, merged, idx, order, rows, table = sort_exchange(keys_loc.reshape(n_dev // LANES, LANES), rows_loc, BASE, RELAY, group_size)
-        own_count = table[OWN, :1]
+        blocks, merged, idx, order, rows, table, own_count, short = sort_exchange(keys_loc.reshape(n_dev // LANES, LANES), rows_loc, BASE, RELAY, group_size)
         idx = idx.reshape(-1)
 
         def arrived():
-            return place(idx, own_count, blocks, width)
+            return place(idx, own_count, blocks, merged, width)
 
         def direct():
             wide = lax.all_to_all(pick(order.reshape(-1), table, rows, cap_rows, group_size), "g", 0, 0, tiled=True)
-            return place(idx, own_count, wide.reshape(-1, *wide.shape[2:]), width)
-
-        merged_rows = lax.cond(table[SHORT, 0] > 0, arrived, direct)
-        return merged.reshape(-1), merged_rows, own_count
+            return place(idx, own_count, wide.reshape(-1, *wide.shape[2:]), merged, width)
+
+        out_rows, out_keys = lax.cond(short[0] > 0, arrived, direct)
+        return out_keys.reshape(-1), out_rows, own_count
 
     row_spec = P(("batch", "g"))
     mat_spec = P(("batch", "g"), None)

time: 119 us -> 120 us (level)
  between operations: 1.32 us -> 2.89 us
where the time goes in v4:
time: 120 us; the launch traced here: 119 us
  Pallas kernels  117 us (98%)
  between operations  2.89 us (2%)
    pallas_call x1, Pallas kernels, sort_exchange(): pl.pallas_call(functools.partial(sort_exchange_kernel, group_size, cap, r...  104 us
    pallas_call x1, Pallas kernels, place(): pl.pallas_call(place_kernel, out_shape=[jax.ShapeDtypeStruct((n_out, widt...  12.3 us

profile of v4, /device:TPU:97, one launch (start us, length us, event | category | flops | bytes accessed | tf_op | source)
XLA Modules:
  0.0 119.4 jit_solution(18113863541465047014)
XLA Ops:
  0.6 104.2 %sort_exchange.1 = (bf16[2144,3,4,128]{3,2,1,0:T(4,128)(2,1)}, f32[32,128]{1,0:T(8,128)S(1)}, s32[32,128]{1,0:T(8,128)S(1)}, s32[16,128]{1,0:T(8,128)S(1)}, bf16...) custom-call(f32[16,128]{1,0:T(8,128)} %bitcast.10, bf16[2048,1536]{1,0:T(8,128)(2,1)} %rows_ref.1), custom_call_target="tpu_custom_call" | custom-call | tf_op jit(solution)/shard_map/sort_exchange/pallas_call | solution.py:330
  105.4 12.3 %conditional.1 = (bf16[4096,1536]{1,0:T(8,128)(2,1)}, f32[4096]{0:T(1024)}) conditional(s32[]{:T(128)} %bitcast.5, (s32[16,128]{1,0:T(8,128)S(1)}, s32[8,128]{1,0:T(8,128)S(1)}, bf16[2048,3,4,128]{3,2,1,0:T(4,128)(2,1)}, s32[4096]{0:T(1024)S(1)}, s32[1]{0:T(128)}, /*index=5*/f32[32,128]{1,0:T(8,128)S(1)}) %tuple.25, (s32[4096]{0:T(1024)S(1)}, ...), branch_computations={%region_0.0_spmd, %region_1.0_spmd} | conditional | bytes 25165840 | solution.py:499
  105.5 12.3 %place_rows.3 = (bf16[4096,1536]{1,0:T(8,128)(2,1)}, f32[32,128]{1,0:T(8,128)}) custom-call(s32[4096]{0:T(1024)S(1)} %get-tuple-element.33.idx_ref, s32[1]{0:T(128)} %get-tuple-element.34.count_ref, bf16[2144,3,4,128]{3,2,1,0:T(4,128)(2,1)} %get-tuple-element.35.in_ref, f32[32,128]{1,0:T(8,128)S(1)} %get-tuple-element.36.keys_ref), custom_call_target="tpu_custom_call" | custom-call | tf_op jit(solution)/shard_map/cond/branch_1_fun/place_rows/pallas_call | solution.py:465

commit v5 on v4

--- a/solution.py
+++ b/solution.py
@@ -242,7 +242,9 @@
     for s in range(1, n // block):
         split(s)
     each(lambda d: share_samples(d).wait())
-    splitters[...] = pick_splitters(samples[:, 0, :])
+    for i in range(group_size):
+        edge_ref[i : i + 1] = samples[i]
+    splitters[...] = pick_splitters(edge_ref[...])
     start_ref[...] = to_table([to_row(count_below(mine[...], splitters[...]), edge_ref.shape)])
     to_starts = pltpu.make_async_copy(start_ref, starts, own_sem.at[3])
     to_starts.start()

time: 120 us -> 117 us (0.975)
  Pallas kernels: 117 us -> 113 us
    pallas_call x1, Pallas kernels: 104 us -> 101 us  [sort_exchange(): pl.pallas_call(functools.partial(sort_exchange_kernel, group_size, cap, r...]
where the time goes in v5:
time: 117 us; the launch traced here: 116 us
  Pallas kernels  113 us (97%)
  between operations  2.89 us (2%)
    pallas_call x1, Pallas kernels, sort_exchange(): pl.pallas_call(functools.partial(sort_exchange_kernel, group_size, cap, r...  101 us
    pallas_call x1, Pallas kernels, place(): pl.pallas_call(place_kernel, out_shape=[jax.ShapeDtypeStruct((n_out, widt...  12.3 us

profile of v5, /device:TPU:97, one launch (start us, length us, event | category | flops | bytes accessed | tf_op | source)
XLA Modules:
  0.0 116.0 jit_solution(10392651911713045716)
XLA Ops:
  0.6 100.8 %sort_exchange.1 = (bf16[2144,3,4,128]{3,2,1,0:T(4,128)(2,1)}, f32[32,128]{1,0:T(8,128)S(1)}, s32[32,128]{1,0:T(8,128)S(1)}, s32[16,128]{1,0:T(8,128)S(1)}, bf16...) custom-call(f32[16,128]{1,0:T(8,128)} %bitcast.10, bf16[2048,1536]{1,0:T(8,128)(2,1)} %rows_ref.1), custom_call_target="tpu_custom_call" | custom-call | tf_op jit(solution)/shard_map/sort_exchange/pallas_call | solution.py:332
  102.0 12.3 %conditional.1 = (bf16[4096,1536]{1,0:T(8,128)(2,1)}, f32[4096]{0:T(1024)}) conditional(s32[]{:T(128)} %bitcast.5, (s32[16,128]{1,0:T(8,128)S(1)}, s32[8,128]{1,0:T(8,128)S(1)}, bf16[2048,3,4,128]{3,2,1,0:T(4,128)(2,1)}, s32[4096]{0:T(1024)S(1)}, s32[1]{0:T(128)}, /*index=5*/f32[32,128]{1,0:T(8,128)S(1)}) %tuple.25, (s32[4096]{0:T(1024)S(1)}, ...), branch_computations={%region_0.0_spmd, %region_1.0_spmd} | conditional | bytes 25165840 | solution.py:501
  102.0 12.3 %place_rows.3 = (bf16[4096,1536]{1,0:T(8,128)(2,1)}, f32[32,128]{1,0:T(8,128)}) custom-call(s32[4096]{0:T(1024)S(1)} %get-tuple-element.33.idx_ref, s32[1]{0:T(128)} %get-tuple-element.34.count_ref, bf16[2144,3,4,128]{3,2,1,0:T(4,128)(2,1)} %get-tuple-element.35.in_ref, f32[32,128]{1,0:T(8,128)S(1)} %get-tuple-element.36.keys_ref), custom_call_target="tpu_custom_call" | custom-call | tf_op jit(solution)/shard_map/cond/branch_1_fun/place_rows/pallas_call | solution.py:467

commit v6 on v5

--- a/solution.py
+++ b/solution.py
@@ -12,7 +12,7 @@
 SUB = 4
 BASE = 65
 RELAY = 2
-WINDOW = 6
+FIRST, SECOND = 12, 22
 SIDE = 4
 CORES = 2
 SLOTS = (((0, 2), (2, 0)), ((0, 1), (2, 3)), ((0, 3), (2, 1)), ((1, 0), (3, 2)), ((3, 0), (1, 2)), ((3, 1), (1, 3)), ((3, 3), (1, 1)), ((2, 2),))
@@ -270,53 +270,56 @@
 
     own_two = pltpu.make_async_copy(second.at[me], out_ref.at[pl.ds(group_size * cap + me * relay, relay)], own_sem.at[1])
     own_base = pltpu.make_async_copy(outgoing.at[me], out_ref.at[pl.ds(me * cap, cap)], own_sem.at[0])
-    gather(far(0))
-    for s in range(group_size - 1):
-        if s >= WINDOW:
-            base(s - WINDOW).wait_send()
-        if s + 1 < group_size - 1:
-            gather(far(s + 1))
-        base(s).start()
-        if s == WINDOW:
-            each(lambda d: share(d).wait())
-            table_ref[...] = make_plan(me, cap, relay * group_size, all_ref, splitters, edge_ref)
-            to_smem = pltpu.make_async_copy(table_ref, table, own_sem.at[5])
-            to_smem.start()
-            gather(me)
-            to_smem.wait()
-        if s == WINDOW + 1:
-            extra = table[EXTRA, 0]
-
-            def gather_extra(b, carry):
-                for u in range(8):
-                    m = b * 8 + u
-                    for r in range(relay):
-                        first[m, r] = row(extra + r * group_size + m)
-                return carry
-
-            lax.fori_loop(0, group_size // 8, gather_extra, 0)
-            arrived[pl.ds(me, 1)] = first[pl.ds(me, 1)]
-            own_base.start()
-        if s == WINDOW + 2:
-            each(lambda d: hop_one(d).start())
-        if s == WINDOW + 4:
-            own_ref[0] = table[OWN, 0]
-            short_ref[0] = table[SHORT, 0]
-            take_segments(cap, relay, table, all_ref, seg_ref, slot_ref)
-            merged_ref[...], idx_ref[...] = bitonic_sort(seg_ref[...], slot_ref[...])
-        if s == WINDOW + 12:
-            each(lambda d: hop_one(d).wait())
-            for j in range(group_size):
-                second[j] = arrived[table[FROM_SRC, j] & (group_size - 1)]
-        if s == WINDOW + 13:
-            each(lambda d: hop_two(d).start())
-            own_two.start()
+
+    def send(begin, end):
+        for s in range(begin, end):
+            gather(far(s))
+            if s > begin:
+                base(s - 1).start()
+        return end - 1
+
+    waiting = send(0, FIRST)
+    gather(me)
+    base(waiting).start()
+    each(lambda d: share(d).wait())
+    table_ref[...] = make_plan(me, cap, relay * group_size, all_ref, splitters, edge_ref)
+    to_smem = pltpu.make_async_copy(table_ref, table, own_sem.at[5])
+    to_smem.start()
+    own_base.start()
+    to_smem.wait()
+    extra = table[EXTRA, 0]
+
+    def gather_extra(b, carry):
+        for u in range(8):
+            m = b * 8 + u
+            for r in range(relay):
+                first[m, r] = row(extra + r * group_size + m)
+        return carry
+
+    lax.fori_loop(0, group_size // 8, gather_extra, 0)
+    arrived[pl.ds(me, 1)] = first[pl.ds(me, 1)]
+    gather(far(FIRST))
+    each(lambda d: hop_one(d).start())
+    base(FIRST).start()
+    waiting = send(FIRST + 1, SECOND)
+    own_ref[0] = table[OWN, 0]
+    short_ref[0] = table[SHORT, 0]
+    take_segments(cap, relay, table, all_ref, seg_ref, slot_ref)
+    base(waiting).start()
+    merged_ref[...], idx_ref[...] = bitonic_sort(seg_ref[...], slot_ref[...])
+    each(lambda d: hop_one(d).wait())
+    for j in range(group_size):
+        second[j] = arrived[table[FROM_SRC, j] & (group_size - 1)]
+    gather(far(SECOND))
+    each(lambda d: hop_two(d).start())
+    own_two.start()
+    base(SECOND).start()
+    waiting = send(SECOND + 1, group_size - 1)
     keep = pltpu.make_async_copy(held, split_ref, own_sem.at[4])
     keep.start()
+    base(waiting).start()
     for s in range(group_size - 1):
-        if s >= group_size - 1 - WINDOW:
-            base(s).wait_send()
-        base(s).wait_recv()
+        base(s).wait()
     each(lambda d: hop_two(d).wait())
     own_two.wait()
     own_base.wait()

time: 117 us -> 116 us (level)
  no operation moved by 1% of the time
where the time goes in v6:
time: 116 us
  Pallas kernels  113 us (97%)
  between operations  2.89 us (2%)
    pallas_call x1, Pallas kernels, sort_exchange(): pl.pallas_call(functools.partial(sort_exchange_kernel, group_size, cap, r...  101 us
    pallas_call x1, Pallas kernels, place(): pl.pallas_call(place_kernel, out_shape=[jax.ShapeDtypeStruct((n_out, widt...  12.3 us

profile of v6, /device:TPU:97, one launch (start us, length us, event | category | flops | bytes accessed | tf_op | source)
XLA Modules:
  0.0 116.0 jit_solution(16868423703559263373)
XLA Ops:
  0.6 100.8 %sort_exchange.1 = (bf16[2144,3,4,128]{3,2,1,0:T(4,128)(2,1)}, f32[32,128]{1,0:T(8,128)S(1)}, s32[32,128]{1,0:T(8,128)S(1)}, s32[16,128]{1,0:T(8,128)S(1)}, bf16...) custom-call(f32[16,128]{1,0:T(8,128)} %bitcast.10, bf16[2048,1536]{1,0:T(8,128)(2,1)} %rows_ref.1), custom_call_target="tpu_custom_call" | custom-call | tf_op jit(solution)/shard_map/sort_exchange/pallas_call | solution.py:335
  102.0 12.3 %conditional.1 = (bf16[4096,1536]{1,0:T(8,128)(2,1)}, f32[4096]{0:T(1024)}) conditional(s32[]{:T(128)} %bitcast.5, (s32[16,128]{1,0:T(8,128)S(1)}, s32[8,128]{1,0:T(8,128)S(1)}, bf16[2048,3,4,128]{3,2,1,0:T(4,128)(2,1)}, s32[4096]{0:T(1024)S(1)}, s32[1]{0:T(128)}, /*index=5*/f32[32,128]{1,0:T(8,128)S(1)}) %tuple.25, (s32[4096]{0:T(1024)S(1)}, ...), branch_computations={%region_0.0_spmd, %region_1.0_spmd} | conditional | bytes 25165840 | solution.py:504
  102.0 12.3 %place_rows.3 = (bf16[4096,1536]{1,0:T(8,128)(2,1)}, f32[32,128]{1,0:T(8,128)}) custom-call(s32[4096]{0:T(1024)S(1)} %get-tuple-element.33.idx_ref, s32[1]{0:T(128)} %get-tuple-element.34.count_ref, bf16[2144,3,4,128]{3,2,1,0:T(4,128)(2,1)} %get-tuple-element.35.in_ref, f32[32,128]{1,0:T(8,128)S(1)} %get-tuple-element.36.keys_ref), custom_call_target="tpu_custom_call" | custom-call | tf_op jit(solution)/shard_map/cond/branch_1_fun/place_rows/pallas_call | solution.py:470

commit v7 on v6

--- a/solution.py
+++ b/solution.py
@@ -12,7 +12,7 @@
 SUB = 4
 BASE = 65
 RELAY = 2
-FIRST, SECOND = 12, 22
+FIRST, SECOND, THIRD = 6, 12, 22
 SIDE = 4
 CORES = 2
 SLOTS = (((0, 2), (2, 0)), ((0, 1), (2, 3)), ((0, 3), (2, 1)), ((1, 0), (3, 2)), ((3, 0), (1, 2)), ((3, 1), (1, 3)), ((3, 3), (1, 1)), ((2, 2),))
@@ -21,8 +21,9 @@
 VMEM = pl.BlockSpec(memory_space=pltpu.VMEM)
 SMEM = pl.BlockSpec(memory_space=pltpu.SMEM)
 ANY = pl.BlockSpec(memory_space=pl.ANY)
+HBM = pl.BlockSpec(memory_space=pltpu.HBM)
 MESH = pl.DeviceIdType.MESH
-STARTS, COL_STARTS, COL_COUNTS, FROM_SRC, EXTRA, SHORT, OWN = range(7)
+FROM_SRC, EXTRA, SHORT, OWN = range(4)
 
 
 def bitonic_sort(keys, vals):
@@ -98,70 +99,58 @@
     return jnp.concatenate([jnp.broadcast_to(r, (1, LANES)) for r in rows], 0).astype(jnp.int32)
 
 
-def make_plan(me, cap, most, all_ref, split_ref, edge_ref):
-    group_size, tiles, _ = all_ref.shape
-    n_dev = tiles * LANES
-    shape = edge_ref.shape
-    lane = lax.broadcasted_iota(jnp.int32, shape, 1)
-    sub = lax.broadcasted_iota(jnp.int32, shape, 0)
-    splitters = split_ref[...]
-    edge_ref[...] = jnp.zeros(shape, jnp.float32)
-
-    def count(b, carry):
-        edges = edge_ref[...]
-        for u in range(4):
-            i = b * 4 + u
-            edges = jnp.where(lane == i, count_below(all_ref[i], splitters), edges)
-        edge_ref[...] = edges
-        return carry
-
-    lax.fori_loop(0, group_size // 4, count, 0)
-    edges = edge_ref[...]
-    after = jnp.concatenate([edges[1:], jnp.full((1, LANES), n_dev, jnp.float32)], 0)
+def make_plan(me, cap, relay, n_dev, edges):
+    group_size = edges.shape[0]
+    lane = lax.broadcasted_iota(jnp.int32, edges.shape, 1)
+    sub = lax.broadcasted_iota(jnp.int32, edges.shape, 0)
+    after = jnp.where(lane == group_size - 1, float(n_dev), pltpu.roll(edges, LANES - 1, 1))
     counts = jnp.where(lane < group_size, after - edges, 0.0)
     over = jnp.maximum(counts - cap, 0.0)
     has = (over > 0).astype(jnp.float32)
     worst = jnp.maximum(jnp.max(jnp.sum(has, axis=0, keepdims=True), axis=1, keepdims=True), jnp.max(jnp.sum(has, axis=1, keepdims=True), axis=0, keepdims=True))
     most_over = jnp.max(jnp.max(over, axis=0, keepdims=True), axis=1, keepdims=True)
-    short = ((worst <= 1) & (most_over <= most)).astype(jnp.float32)
-    mine = lane == me
-    starts = to_row(jnp.sum(jnp.where(mine, edges, 0.0), axis=1, keepdims=True), shape)
-    col_starts = jnp.sum(jnp.where(sub == me, edges, 0.0), axis=0, keepdims=True)
-    col_counts = jnp.sum(jnp.where(sub == me, counts, 0.0), axis=0, keepdims=True)
-    from_src = to_row(jnp.sum(has * lane.astype(jnp.float32), axis=1, keepdims=True), shape)
-    extra = jnp.sum(jnp.sum(jnp.where(mine, has * (edges + cap), 0.0), axis=0, keepdims=True), axis=1, keepdims=True)
-    own = jnp.sum(col_counts, axis=1, keepdims=True)
-    return to_table([starts, col_starts, col_counts, from_src, extra, short, own])
-
-
-def take_segments(cap, relay, table_ref, all_ref, out_ref, slot_ref):
-    group_size, tiles, _ = all_ref.shape
+    short = ((worst <= 1) & (most_over <= relay * group_size)).astype(jnp.float32)
+    my_counts = jnp.sum(jnp.where(lane == me, counts, 0.0), axis=1, keepdims=True)
+    own = jnp.sum(my_counts, axis=0, keepdims=True)
+    from_src = jnp.sum(has * sub.astype(jnp.float32), axis=0, keepdims=True)
+    extra = jnp.sum(jnp.sum(jnp.where(sub == me, has * (edges + cap), 0.0), axis=0, keepdims=True), axis=1, keepdims=True)
+    past = lane - cap
+    slot = jnp.where(past < 0, sub * cap + lane, group_size * cap + lax.rem(past, group_size) * relay + past // group_size)
+    slot = jnp.where(lane.astype(jnp.float32) < my_counts, slot, 0)
+    return to_table([from_src, extra, short, own]), slot
+
+
+def write_messages(start_ref, mine, msg_ref, edges):
+    group_size = msg_ref.shape[0]
+    tiles = mine.shape[0]
+    n_dev = tiles * LANES
     lane = lax.broadcasted_iota(jnp.int32, (1, LANES), 1)
-    short = table_ref[SHORT, 0] > 0
-    past = lane - cap
-    relayed = group_size * cap + lax.rem(past, group_size) * relay + past // group_size
-    unused = jnp.where(short, group_size * (cap + relay), group_size * LANES)
-    for i in range(group_size):
-        s = jnp.clip(table_ref[COL_STARTS, i], 0, tiles * LANES - 1)
+
+    def one(j):
+        s = start_ref[0, j] & (2 * n_dev - 1)
+        stop = jnp.where(j == group_size - 1, n_dev, start_ref[0, j + 1])
         t = s // LANES
-        off = s - t * LANES
-        a = all_ref[i, pl.ds(t, 1), :]
-        b = all_ref[i, pl.ds(jnp.minimum(t + 1, tiles - 1), 1), :]
-        shift = lax.rem(LANES - off, LANES)
-        a = pltpu.roll(a, shift, 1)
-        b = pltpu.roll(b, shift, 1)
-        v = jnp.where(lane < LANES - off, a, b)
-        live = lane < table_ref[COL_COUNTS, i]
-        out_ref[pl.ds(i, 1), :] = jnp.where(live, v, PAD_KEY)
-        slot = jnp.where(short, jnp.where(past < 0, i * cap + lane, relayed), i * LANES + lane)
-        slot_ref[pl.ds(i, 1), :] = jnp.where(live, slot, unused)
+        off = s & (LANES - 1)
+        a = mine[pl.ds(jnp.minimum(t, tiles - 1), 1), :]
+        b = mine[pl.ds(jnp.minimum(t + 1, tiles - 1), 1), :]
+        shift = (LANES - off) & (LANES - 1)
+        v = jnp.where(lane < LANES - off, pltpu.roll(a, shift, 1), pltpu.roll(b, shift, 1))
+        msg_ref[j, 0:1] = jnp.where(lane < stop - s, v, PAD_KEY)
+        msg_ref[j, 1:2] = edges
+
+    def body(b, carry):
+        for u in range(4):
+            one(b * 4 + u)
+        return carry
+
+    lax.fori_loop(0, group_size // 4, body, 0)
 
 
 def sort_exchange_kernel(
     group_size, cap, relay, block,
     keys_ref, rows_ref,
-    out_ref, merged_ref, idx_ref, order_ref, split_ref, table_ref, own_ref, short_ref,
-    fetched, held, outgoing, first, arrived, second, mine, all_ref, my_samples, samples, start_ref, splitters, edge_ref, seg_ref, slot_ref, order, starts, table,
+    out_ref, merged_ref, idx_ref, order_ref, split_ref, start_ref, seg_ref, own_ref, short_ref,
+    fetched, held, outgoing, first, arrived, second, mine, my_samples, samples, msgs, inbox, edge_ref, edge_row, table_ref, order, starts, table,
     in_sem, own_sem, send_sem, recv_sem,
 ):
     me = lax.axis_index("g")
@@ -198,7 +187,6 @@
     sorted_keys, sorted_places = bitonic_sort(keys_ref[...], places)
     mine[...] = sorted_keys
     order_ref[...] = sorted_places
-    all_ref[pl.ds(me, 1)] = sorted_keys[None]
     my_samples[...] = sample_row(sorted_keys, group_size)
     samples[pl.ds(me, 1)] = my_samples[...][None]
     split(0)
@@ -210,7 +198,7 @@
         )
 
     def share(d):
-        return remote(d, peer(d), mine, all_ref.at[me], 3)
+        return remote(d, peer(d), msgs.at[peer(d)], inbox.at[me], 3)
 
     def share_samples(d):
         return remote(d, peer(d), my_samples, samples.at[me], 4)
@@ -236,7 +224,6 @@
         lax.fori_loop(1, group_size, body, 0)
 
     each(lambda d: share_samples(d).start())
-    each(lambda d: share(d).start())
     to_order = pltpu.make_async_copy(order_ref, order, own_sem.at[2])
     to_order.start()
     for s in range(1, n // block):
@@ -244,8 +231,9 @@
     each(lambda d: share_samples(d).wait())
     for i in range(group_size):
         edge_ref[i : i + 1] = samples[i]
-    splitters[...] = pick_splitters(edge_ref[...])
-    start_ref[...] = to_table([to_row(count_below(mine[...], splitters[...]), edge_ref.shape)])
+    edges = to_row(count_below(mine[...], pick_splitters(edge_ref[...])), edge_ref.shape)
+    edge_row[...] = edges
+    start_ref[...] = to_table([edges])
     to_starts = pltpu.make_async_copy(start_ref, starts, own_sem.at[3])
     to_starts.start()
     to_order.wait()
@@ -258,7 +246,7 @@
         return held[order[k >> 7, k & (LANES - 1)] & last]
 
     def gather(dst):
-        begin = starts[STARTS, dst]
+        begin = starts[0, dst]
 
         def body(b, carry):
             for u in range(13):
@@ -279,10 +267,20 @@
         return end - 1
 
     waiting = send(0, FIRST)
+    write_messages(starts, mine, msgs, edge_row[...])
+    base(waiting).start()
+    inbox[pl.ds(me, 1)] = msgs[pl.ds(me, 1)]
+    gather(far(FIRST))
+    each(lambda d: share(d).start())
+    base(FIRST).start()
+    waiting = send(FIRST + 1, SECOND)
     gather(me)
     base(waiting).start()
     each(lambda d: share(d).wait())
-    table_ref[...] = make_plan(me, cap, relay * group_size, all_ref, splitters, edge_ref)
+    for i in range(group_size):
+        seg_ref[i : i + 1] = inbox[i, 0:1]
+        edge_ref[i : i + 1] = inbox[i, 1:2]
+    table_ref[...], slots = make_plan(me, cap, relay, n, edge_ref[...])
     to_smem = pltpu.make_async_copy(table_ref, table, own_sem.at[5])
     to_smem.start()
     own_base.start()
@@ -298,23 +296,22 @@
 
     lax.fori_loop(0, group_size // 8, gather_extra, 0)
     arrived[pl.ds(me, 1)] = first[pl.ds(me, 1)]
-    gather(far(FIRST))
+    gather(far(SECOND))
     each(lambda d: hop_one(d).start())
-    base(FIRST).start()
-    waiting = send(FIRST + 1, SECOND)
+    base(SECOND).start()
+    waiting = send(SECOND + 1, THIRD)
     own_ref[0] = table[OWN, 0]
     short_ref[0] = table[SHORT, 0]
-    take_segments(cap, relay, table, all_ref, seg_ref, slot_ref)
     base(waiting).start()
-    merged_ref[...], idx_ref[...] = bitonic_sort(seg_ref[...], slot_ref[...])
+    merged_ref[...], idx_ref[...] = bitonic_sort(seg_ref[...], slots)
     each(lambda d: hop_one(d).wait())
     for j in range(group_size):
         second[j] = arrived[table[FROM_SRC, j] & (group_size - 1)]
-    gather(far(SECOND))
+    gather(far(THIRD))
     each(lambda d: hop_two(d).start())
     own_two.start()
-    base(SECOND).start()
-    waiting = send(SECOND + 1, group_size - 1)
+    base(THIRD).start()
+    waiting = send(THIRD + 1, group_size - 1)
     keep = pltpu.make_async_copy(held, split_ref, own_sem.at[4])
     keep.start()
     base(waiting).start()
@@ -335,17 +332,18 @@
     return pl.pallas_call(
         functools.partial(sort_exchange_kernel, group_size, cap, relay, block),
         out_shape=[
-            jax.ShapeDtypeStruct((group_size * (cap + relay), *row), rows.dtype),
+            pltpu.VMEM((group_size * (cap + relay), *row), rows.dtype),
             jax.ShapeDtypeStruct(segs, keys.dtype),
-            jax.ShapeDtypeStruct(segs, jnp.int32),
+            pltpu.VMEM(segs, jnp.int32),
             jax.ShapeDtypeStruct(keys.shape, jnp.int32),
             jax.ShapeDtypeStruct((n, *row), rows.dtype),
             jax.ShapeDtypeStruct((8, LANES), jnp.int32),
+            jax.ShapeDtypeStruct(segs, keys.dtype),
             jax.ShapeDtypeStruct((1,), jnp.int32),
             jax.ShapeDtypeStruct((1,), jnp.int32),
         ],
-        in_specs=[VMEM, ANY],
-        out_specs=[ANY, VMEM, VMEM, VMEM, ANY, VMEM, SMEM, SMEM],
+        in_specs=[VMEM, HBM],
+        out_specs=[VMEM, VMEM, VMEM, VMEM, HBM, VMEM, VMEM, SMEM, SMEM],
         scratch_shapes=[
             pltpu.VMEM((n // block, block, width), rows.dtype),
             pltpu.VMEM((n, *row), rows.dtype),
@@ -354,14 +352,13 @@
             pltpu.VMEM((group_size, relay, *row), rows.dtype),
             pltpu.VMEM((group_size, relay, *row), rows.dtype),
             pltpu.VMEM(keys.shape, keys.dtype),
-            pltpu.VMEM((group_size, *keys.shape), keys.dtype),
             pltpu.VMEM((1, LANES), keys.dtype),
             pltpu.VMEM((group_size, 1, LANES), keys.dtype),
+            pltpu.VMEM((group_size, 2, LANES), keys.dtype),
+            pltpu.VMEM((group_size, 2, LANES), keys.dtype),
+            pltpu.VMEM(segs, jnp.float32),
+            pltpu.VMEM((1, LANES), jnp.float32),
             pltpu.VMEM((8, LANES), jnp.int32),
-            pltpu.VMEM(segs, keys.dtype),
-            pltpu.VMEM(segs, jnp.float32),
-            pltpu.VMEM(segs, keys.dtype),
-            pltpu.VMEM(segs, jnp.int32),
             pltpu.SMEM(keys.shape, jnp.int32),
             pltpu.SMEM((8, LANES), jnp.int32),
             pltpu.SMEM((8, LANES), jnp.int32),
@@ -370,7 +367,7 @@
             sems((5, group_size)),
             sems((5, group_size)),
         ],
-        compiler_params=pltpu.CompilerParams(collective_id=0, has_side_effects=True),
+        compiler_params=pltpu.CompilerParams(collective_id=0, has_side_effects=True, vmem_limit_bytes=52 * 1024 * 1024),
         name="sort_exchange",
     )(keys, rows)
 
@@ -379,7 +376,7 @@
     last = rows_ref.shape[0] - 1
 
     def per_dst(j, carry):
-        first = table_ref[STARTS, j]
+        first = table_ref[0, j]
 
         def body(b, c):
             for u in range(8):
@@ -402,17 +399,14 @@
     )(order, table, rows)
 
 
-def place_kernel(idx_ref, count_ref, in_ref, keys_ref, out_ref, out_keys_ref, held, staged, blank, in_sem, out_sem, blank_sem):
+def place_kernel(idx_ref, count_ref, held, keys_ref, out_ref, out_keys_ref, staged, blank, out_sem, blank_sem):
     slots, block, width = staged.shape
-    total = in_ref.shape[0]
     parts = held.shape[1]
-    load = pltpu.make_async_copy(in_ref, held.at[pl.ds(0, total)], in_sem)
-    load.start()
     out_keys_ref[...] = keys_ref[...]
     blank[...] = jnp.zeros(blank.shape, blank.dtype)
-    held[total] = jnp.zeros(held.shape[1:], held.dtype)
     steps = out_ref.shape[0] // block
-    live = pl.cdiv(count_ref[0], block)
+    count = count_ref[0]
+    live = pl.cdiv(count, block)
 
     def clear(s):
         return pltpu.make_async_copy(blank, out_ref.at[pl.ds(s * block, block)], blank_sem)
@@ -421,13 +415,9 @@
         slot = lax.rem(s, slots)
         return pltpu.make_async_copy(staged.at[slot], out_ref.at[pl.ds(s * block, block)], out_sem.at[slot])
 
-    load.wait()
-
     def start_clear(s, carry):
         clear(s).start()
         return carry
-
-    lax.fori_loop(live, steps, start_clear, 0)
 
     def step(s, carry):
         @pl.when(s >= slots)
@@ -446,10 +436,18 @@
             return c
 
         lax.fori_loop(0, block // 16, body, 0)
+
+        @pl.when((s + 1) * block > count)
+        def _():
+            row = lax.broadcasted_iota(jnp.int32, (block, width), 0) + s * block
+            staged[slot] = jnp.where(row < count, staged[slot], jnp.zeros((block, width), staged.dtype))
+
         store(s).start()
         return carry
 
-    lax.fori_loop(0, live, step, 0)
+    lax.fori_loop(0, jnp.minimum(live, 1), step, 0)
+    lax.fori_loop(live, steps, start_clear, 0)
+    lax.fori_loop(1, live, step, 0)
 
     def end_store(s, carry):
         store(s).wait()
@@ -470,16 +468,15 @@
     return pl.pallas_call(
         place_kernel,
         out_shape=[jax.ShapeDtypeStruct((n_out, width), rows.dtype), jax.ShapeDtypeStruct(keys.shape, keys.dtype)],
-        in_specs=[SMEM, SMEM, ANY, VMEM],
+        in_specs=[SMEM, SMEM, VMEM, VMEM],
         out_specs=[ANY, VMEM],
         scratch_shapes=[
-            pltpu.VMEM((rows.shape[0] + 1, *rows.shape[1:]), rows.dtype),
             pltpu.VMEM((slots, block, width), rows.dtype),
             pltpu.VMEM((block, width), rows.dtype),
-            pltpu.SemaphoreType.DMA,
             pltpu.SemaphoreType.DMA((slots,)),
             pltpu.SemaphoreType.DMA,
         ],
+        compiler_params=pltpu.CompilerParams(vmem_limit_bytes=24 * 1024 * 1024),
         name="place_rows",
     )(idx, count, rows, keys)
 
@@ -491,17 +488,15 @@
         n_dev = keys_loc.shape[0]
         width = rows_loc.shape[1]
         cap_rows = 2 * n_dev // group_size
-        blocks, merged, idx, order, rows, table, own_count, short = sort_exchange(keys_loc.reshape(n_dev // LANES, LANES), rows_loc, BASE, RELAY, group_size)
-        idx = idx.reshape(-1)
-
-        def arrived():
-            return place(idx, own_count, blocks, merged, width)
-
-        def direct():
-            wide = lax.all_to_all(pick(order.reshape(-1), table, rows, cap_rows, group_size), "g", 0, 0, tiled=True)
-            return place(idx, own_count, wide.reshape(-1, *wide.shape[2:]), merged, width)
-
-        out_rows, out_keys = lax.cond(short[0] > 0, arrived, direct)
+        blocks, merged, idx, order, rows, starts, segs, own_count, short = sort_exchange(keys_loc.reshape(n_dev // LANES, LANES), rows_loc, BASE, RELAY, group_size)
+        out_rows, out_keys = place(idx.reshape(-1), own_count, blocks, merged, width)
+
+        def general(carry):
+            wide = lax.all_to_all(pick(order.reshape(-1), starts, rows, cap_rows, group_size), "g", 0, 0, tiled=True)
+            _, at = lax.sort((segs.reshape(-1), lax.iota(jnp.int32, segs.size)), num_keys=1)
+            return jnp.int32(1), place(at, own_count, wide.reshape(-1, *wide.shape[2:]), merged, width)[0]
+
+        _, out_rows = lax.while_loop(lambda carry: carry[0] == 0, general, (short[0], out_rows))
         return out_keys.reshape(-1), out_rows, own_count
 
     row_spec = P(("batch", "g"))

time: 116 us -> 115 us (level); the launches traced: 116 us -> 113 us
  Pallas kernels: 113 us -> 110 us
    pallas_call x1, Pallas kernels: 12.3 us -> 9.49 us  [place(): pl.pallas_call(place_kernel, out_shape=[jax.ShapeDtypeStruct((n_out, widt...]
where the time goes in v7:
time: 115 us; the launch traced here: 113 us
  Pallas kernels  110 us (96%)
  between operations  2.39 us (2%)
    pallas_call x1, Pallas kernels, sort_exchange(): pl.pallas_call(functools.partial(sort_exchange_kernel, group_size, cap, r...  101 us
    pallas_call x1, Pallas kernels, place(): pl.pallas_call(place_kernel, out_shape=[jax.ShapeDtypeStruct((n_out, widt...  9.49 us

profile of v7, /device:TPU:97, one launch (start us, length us, event | category | flops | bytes accessed | tf_op | source)
XLA Modules:
  0.0 112.9 jit_solution(4959956568868966099)
XLA Ops:
  0.6 100.5 %sort_exchange.1 = (bf16[2144,3,4,128]{3,2,1,0:T(4,128)(2,1)S(1)}, f32[32,128]{1,0:T(8,128)S(1)}, s32[32,128]{1,0:T(8,128)S(1)}, s32[16,128]{1,0:T(8,128)S(1)}, ...) custom-call(f32[16,128]{1,0:T(8,128)} %bitcast.10, ...), custom_call_target="tpu_custom_call" | custom-call | tf_op jit(solution)/shard_map/sort_exchange/pallas_call | solution.py:332
  101.1 9.5 %place_rows.3 = (bf16[4096,1536]{1,0:T(8,128)(2,1)}, f32[32,128]{1,0:T(8,128)}) custom-call(s32[4096]{0:T(1024)S(1)} %bitcast.7, s32[1]{0:T(128)} %get-tuple-element.127.count_ref, bf16[2144,3,4,128]{3,2,1,0:T(4,128)(2,1)S(1)} %get-tuple-element.58.held, f32[32,128]{1,0:T(8,128)S(1)} %get-tuple-element.105.keys_ref), custom_call_target="tpu_custom_call" | custom-call | tf_op jit(solution)/shard_map/place_rows/pallas_call | solution.py:468
  110.6 0.6 while.9

commit v8 on v7

--- a/solution.py
+++ b/solution.py
@@ -12,7 +12,7 @@
 SUB = 4
 BASE = 65
 RELAY = 2
-FIRST, SECOND, THIRD = 6, 12, 22
+FIRST, LATE = 12, 27
 SIDE = 4
 CORES = 2
 SLOTS = (((0, 2), (2, 0)), ((0, 1), (2, 3)), ((0, 3), (2, 1)), ((1, 0), (3, 2)), ((3, 0), (1, 2)), ((3, 1), (1, 3)), ((3, 3), (1, 1)), ((2, 2),))
@@ -120,7 +120,7 @@
     return to_table([from_src, extra, short, own]), slot
 
 
-def write_messages(start_ref, mine, msg_ref, edges):
+def write_segments(start_ref, mine, msg_ref):
     group_size = msg_ref.shape[0]
     tiles = mine.shape[0]
     n_dev = tiles * LANES
@@ -135,8 +135,7 @@
         b = mine[pl.ds(jnp.minimum(t + 1, tiles - 1), 1), :]
         shift = (LANES - off) & (LANES - 1)
         v = jnp.where(lane < LANES - off, pltpu.roll(a, shift, 1), pltpu.roll(b, shift, 1))
-        msg_ref[j, 0:1] = jnp.where(lane < stop - s, v, PAD_KEY)
-        msg_ref[j, 1:2] = edges
+        msg_ref[j] = jnp.where(lane < stop - s, v, PAD_KEY)
 
     def body(b, carry):
         for u in range(4):
@@ -150,7 +149,7 @@
     group_size, cap, relay, block,
     keys_ref, rows_ref,
     out_ref, merged_ref, idx_ref, order_ref, split_ref, start_ref, seg_ref, own_ref, short_ref,
-    fetched, held, outgoing, first, arrived, second, mine, my_samples, samples, msgs, inbox, edge_ref, edge_row, table_ref, order, starts, table,
+    fetched, held, outgoing, first, arrived, second, mine, my_samples, samples, msgs, inbox, all_edges, edge_ref, edge_row, table_ref, slot_ref, order, starts, table,
     in_sem, own_sem, send_sem, recv_sem,
 ):
     me = lax.axis_index("g")
@@ -199,6 +198,9 @@
 
     def share(d):
         return remote(d, peer(d), msgs.at[peer(d)], inbox.at[me], 3)
+
+    def share_edges(d):
+        return remote(d, peer(d), edge_row, all_edges.at[me], 5)
 
     def share_samples(d):
         return remote(d, peer(d), my_samples, samples.at[me], 4)
@@ -235,9 +237,11 @@
     edge_row[...] = edges
     start_ref[...] = to_table([edges])
     to_starts = pltpu.make_async_copy(start_ref, starts, own_sem.at[3])
+    all_edges[pl.ds(me, 1)] = edges[None]
     to_starts.start()
     to_order.wait()
     to_starts.wait()
+    each(lambda d: share_edges(d).start())
 
     last = n - 1
 
@@ -267,23 +271,18 @@
         return end - 1
 
     waiting = send(0, FIRST)
-    write_messages(starts, mine, msgs, edge_row[...])
+    write_segments(starts, mine, msgs)
     base(waiting).start()
     inbox[pl.ds(me, 1)] = msgs[pl.ds(me, 1)]
-    gather(far(FIRST))
-    each(lambda d: share(d).start())
-    base(FIRST).start()
-    waiting = send(FIRST + 1, SECOND)
-    gather(me)
-    base(waiting).start()
-    each(lambda d: share(d).wait())
+    each(lambda d: share_edges(d).wait())
     for i in range(group_size):
-        seg_ref[i : i + 1] = inbox[i, 0:1]
-        edge_ref[i : i + 1] = inbox[i, 1:2]
+        edge_ref[i : i + 1] = all_edges[i]
     table_ref[...], slots = make_plan(me, cap, relay, n, edge_ref[...])
+    slot_ref[...] = slots
     to_smem = pltpu.make_async_copy(table_ref, table, own_sem.at[5])
     to_smem.start()
-    own_base.start()
+    gather(far(FIRST))
+    base(FIRST).start()
     to_smem.wait()
     extra = table[EXTRA, 0]
 
@@ -296,25 +295,31 @@
 
     lax.fori_loop(0, group_size // 8, gather_extra, 0)
     arrived[pl.ds(me, 1)] = first[pl.ds(me, 1)]
-    gather(far(SECOND))
+    gather(far(FIRST + 1))
     each(lambda d: hop_one(d).start())
-    base(SECOND).start()
-    waiting = send(SECOND + 1, THIRD)
+    each(lambda d: share(d).start())
+    base(FIRST + 1).start()
+    waiting = send(FIRST + 2, LATE)
+    gather(me)
+    base(waiting).start()
+    for s in range(LATE, group_size - 1):
+        gather(far(s))
+    own_base.start()
     own_ref[0] = table[OWN, 0]
     short_ref[0] = table[SHORT, 0]
-    base(waiting).start()
-    merged_ref[...], idx_ref[...] = bitonic_sort(seg_ref[...], slots)
+    each(lambda d: share(d).wait())
+    for i in range(group_size):
+        seg_ref[i : i + 1] = inbox[i]
     each(lambda d: hop_one(d).wait())
     for j in range(group_size):
         second[j] = arrived[table[FROM_SRC, j] & (group_size - 1)]
-    gather(far(THIRD))
+    merged_ref[...], idx_ref[...] = bitonic_sort(seg_ref[...], slot_ref[...])
     each(lambda d: hop_two(d).start())
     own_two.start()
-    base(THIRD).start()
-    waiting = send(THIRD + 1, group_size - 1)
+    for s in range(LATE, group_size - 1):
+        base(s).start()
     keep = pltpu.make_async_copy(held, split_ref, own_sem.at[4])
     keep.start()
-    base(waiting).start()
     for s in range(group_size - 1):
         base(s).wait()
     each(lambda d: hop_two(d).wait())
@@ -354,18 +359,20 @@
             pltpu.VMEM(keys.shape, keys.dtype),
             pltpu.VMEM((1, LANES), keys.dtype),
             pltpu.VMEM((group_size, 1, LANES), keys.dtype),
-            pltpu.VMEM((group_size, 2, LANES), keys.dtype),
-            pltpu.VMEM((group_size, 2, LANES), keys.dtype),
+            pltpu.VMEM((group_size, 1, LANES), keys.dtype),
+            pltpu.VMEM((group_size, 1, LANES), keys.dtype),
+            pltpu.VMEM((group_size, 1, LANES), jnp.float32),
             pltpu.VMEM(segs, jnp.float32),
             pltpu.VMEM((1, LANES), jnp.float32),
             pltpu.VMEM((8, LANES), jnp.int32),
+            pltpu.VMEM(segs, jnp.int32),
             pltpu.SMEM(keys.shape, jnp.int32),
             pltpu.SMEM((8, LANES), jnp.int32),
             pltpu.SMEM((8, LANES), jnp.int32),
             sems((n // block,)),
             sems((6,)),
-            sems((5, group_size)),
-            sems((5, group_size)),
+            sems((6, group_size)),
+            sems((6, group_size)),
         ],
         compiler_params=pltpu.CompilerParams(collective_id=0, has_side_effects=True, vmem_limit_bytes=52 * 1024 * 1024),
         name="sort_exchange",

time: 115 us -> 116 us (level); the launches traced: 113 us -> 116 us
  Pallas kernels: 110 us -> 113 us
    pallas_call x1, Pallas kernels: 101 us -> 104 us  [sort_exchange(): pl.pallas_call(functools.partial(sort_exchange_kernel, group_size, cap, r...]
where the time goes in v8:
time: 116 us
  Pallas kernels  113 us (97%)
  between operations  2.39 us (2%)
    pallas_call x1, Pallas kernels, sort_exchange(): pl.pallas_call(functools.partial(sort_exchange_kernel, group_size, cap, r...  104 us
    pallas_call x1, Pallas kernels, place(): pl.pallas_call(place_kernel, out_shape=[jax.ShapeDtypeStruct((n_out, widt...  9.49 us

profile of v8, /device:TPU:97, one launch (start us, length us, event | category | flops | bytes accessed | tf_op | source)
XLA Modules:
  0.0 115.9 jit_solution(16772917225588918253)
XLA Ops:
  0.6 103.5 %sort_exchange.1 = (bf16[2144,3,4,128]{3,2,1,0:T(4,128)(2,1)S(1)}, f32[32,128]{1,0:T(8,128)S(1)}, s32[32,128]{1,0:T(8,128)S(1)}, s32[16,128]{1,0:T(8,128)S(1)}, ...) custom-call(f32[16,128]{1,0:T(8,128)} %bitcast.10, ...), custom_call_target="tpu_custom_call" | custom-call | tf_op jit(solution)/shard_map/sort_exchange/pallas_call | solution.py:337
  104.1 9.5 %place_rows.3 = (bf16[4096,1536]{1,0:T(8,128)(2,1)}, f32[32,128]{1,0:T(8,128)}) custom-call(s32[4096]{0:T(1024)S(1)} %bitcast.7, s32[1]{0:T(128)} %get-tuple-element.127.count_ref, bf16[2144,3,4,128]{3,2,1,0:T(4,128)(2,1)S(1)} %get-tuple-element.58.held, f32[32,128]{1,0:T(8,128)S(1)} %get-tuple-element.105.keys_ref), custom_call_target="tpu_custom_call" | custom-call | tf_op jit(solution)/shard_map/place_rows/pallas_call | solution.py:475
  113.6 0.6 while.9

commit v9 on v7

--- a/solution.py
+++ b/solution.py
@@ -11,12 +11,12 @@
 LANES = 128
 SUB = 4
 BASE = 65
-RELAY = 2
+RELAY = 4
 FIRST, SECOND, THIRD = 6, 12, 22
 SIDE = 4
 CORES = 2
 SLOTS = (((0, 2), (2, 0)), ((0, 1), (2, 3)), ((0, 3), (2, 1)), ((1, 0), (3, 2)), ((3, 0), (1, 2)), ((3, 1), (1, 3)), ((3, 3), (1, 1)), ((2, 2),))
-STEPS = ((0, 0, 1), *((dx, dy, dc) for slot in SLOTS for dc in (1, 0) for dx, dy in slot))
+STEPS = (*((dx, dy, dc) for slot in SLOTS for dc in (1, 0) for dx, dy in slot), (0, 0, 1))
 
 VMEM = pl.BlockSpec(memory_space=pltpu.VMEM)
 SMEM = pl.BlockSpec(memory_space=pltpu.SMEM)
@@ -101,6 +101,7 @@
 
 def make_plan(me, cap, relay, n_dev, edges):
     group_size = edges.shape[0]
+    hubs = group_size // CORES
     lane = lax.broadcasted_iota(jnp.int32, edges.shape, 1)
     sub = lax.broadcasted_iota(jnp.int32, edges.shape, 0)
     after = jnp.where(lane == group_size - 1, float(n_dev), pltpu.roll(edges, LANES - 1, 1))
@@ -109,13 +110,13 @@
     has = (over > 0).astype(jnp.float32)
     worst = jnp.maximum(jnp.max(jnp.sum(has, axis=0, keepdims=True), axis=1, keepdims=True), jnp.max(jnp.sum(has, axis=1, keepdims=True), axis=0, keepdims=True))
     most_over = jnp.max(jnp.max(over, axis=0, keepdims=True), axis=1, keepdims=True)
-    short = ((worst <= 1) & (most_over <= relay * group_size)).astype(jnp.float32)
+    short = ((worst <= 1) & (most_over <= relay * hubs)).astype(jnp.float32)
     my_counts = jnp.sum(jnp.where(lane == me, counts, 0.0), axis=1, keepdims=True)
     own = jnp.sum(my_counts, axis=0, keepdims=True)
     from_src = jnp.sum(has * sub.astype(jnp.float32), axis=0, keepdims=True)
     extra = jnp.sum(jnp.sum(jnp.where(sub == me, has * (edges + cap), 0.0), axis=0, keepdims=True), axis=1, keepdims=True)
     past = lane - cap
-    slot = jnp.where(past < 0, sub * cap + lane, group_size * cap + lax.rem(past, group_size) * relay + past // group_size)
+    slot = jnp.where(past < 0, sub * cap + lane, group_size * cap + lax.rem(past, hubs) * relay + past // hubs)
     slot = jnp.where(lane.astype(jnp.float32) < my_counts, slot, 0)
     return to_table([from_src, extra, short, own]), slot
 
@@ -189,7 +190,6 @@
     order_ref[...] = sorted_places
     my_samples[...] = sample_row(sorted_keys, group_size)
     samples[pl.ds(me, 1)] = my_samples[...][None]
-    split(0)
     pl.semaphore_wait(barrier, group_size - 1)
 
     def remote(d, dst, src_ref, dst_ref, kind):
@@ -203,11 +203,32 @@
     def share_samples(d):
         return remote(d, peer(d), my_samples, samples.at[me], 4)
 
-    def hop_one(d):
-        return remote(d, peer(d), first.at[peer(d)], arrived.at[me], 1)
-
-    def hop_two(d):
-        return remote(d, peer(d), second.at[peer(d)], out_ref.at[pl.ds(group_size * cap + me * relay, relay)], 2)
+    hubs = group_size // CORES
+    chip = me // CORES
+    forward = core == CORES - 1
+
+    def near(d):
+        return lax.rem(chip + d, hubs)
+
+    def hop_one(d, c):
+        return pltpu.make_async_remote_copy(
+            src_ref=first.at[near(d)],
+            dst_ref=arrived.at[me],
+            send_sem=send_sem.at[1, d],
+            recv_sem=recv_sem.at[1, c * hubs + d],
+            device_id={"g": near(d) * CORES + CORES - 1},
+            device_id_type=MESH,
+        )
+
+    def hop_two(d, hub):
+        return pltpu.make_async_remote_copy(
+            src_ref=second.at[peer(d)],
+            dst_ref=out_ref.at[pl.ds(group_size * cap + chip * relay, relay)],
+            send_sem=send_sem.at[2, d],
+            recv_sem=recv_sem.at[2, hub],
+            device_id={"g": peer(d)},
+            device_id_type=MESH,
+        )
 
     def far(s):
         dx, dy, dc = STEPS[s]
@@ -216,17 +237,17 @@
     def base(s):
         return remote(s, far(s), outgoing.at[far(s)], out_ref.at[pl.ds(me * cap, cap)], 0)
 
-    def each(act):
+    def each(act, begin=1, end=group_size):
         def body(d, carry):
             act(d)
             return carry
 
-        lax.fori_loop(1, group_size, body, 0)
+        lax.fori_loop(begin, end, body, 0)
 
     each(lambda d: share_samples(d).start())
     to_order = pltpu.make_async_copy(order_ref, order, own_sem.at[2])
     to_order.start()
-    for s in range(1, n // block):
+    for s in range(n // block):
         split(s)
     each(lambda d: share_samples(d).wait())
     for i in range(group_size):
@@ -256,7 +277,6 @@
 
         lax.fori_loop(0, cap // 13, body, 0)
 
-    own_two = pltpu.make_async_copy(second.at[me], out_ref.at[pl.ds(group_size * cap + me * relay, relay)], own_sem.at[1])
     own_base = pltpu.make_async_copy(outgoing.at[me], out_ref.at[pl.ds(me * cap, cap)], own_sem.at[0])
 
     def send(begin, end):
@@ -288,28 +308,48 @@
     extra = table[EXTRA, 0]
 
     def gather_extra(b, carry):
-        for u in range(8):
-            m = b * 8 + u
+        for u in range(4):
+            m = b * 4 + u
             for r in range(relay):
-                first[m, r] = row(extra + r * group_size + m)
+                first[m, r] = row(extra + r * hubs + m)
         return carry
 
-    lax.fori_loop(0, group_size // 8, gather_extra, 0)
-    arrived[pl.ds(me, 1)] = first[pl.ds(me, 1)]
+    lax.fori_loop(0, hubs // 4, gather_extra, 0)
     gather(far(SECOND))
-    each(lambda d: hop_one(d).start())
+    each(lambda d: hop_one(d, core).start(), 1, hubs)
+
+    @pl.when(jnp.logical_not(forward))
+    def _():
+        hop_one(0, 0).start()
+
+    @pl.when(forward)
+    def _():
+        arrived[me] = first[chip]
+
     base(SECOND).start()
     waiting = send(SECOND + 1, THIRD)
     own_ref[0] = table[OWN, 0]
     short_ref[0] = table[SHORT, 0]
     base(waiting).start()
     merged_ref[...], idx_ref[...] = bitonic_sort(seg_ref[...], slots)
-    each(lambda d: hop_one(d).wait())
-    for j in range(group_size):
-        second[j] = arrived[table[FROM_SRC, j] & (group_size - 1)]
     gather(far(THIRD))
-    each(lambda d: hop_two(d).start())
-    own_two.start()
+    each(lambda d: hop_one(d, core).wait_send(), 1, hubs)
+
+    @pl.when(jnp.logical_not(forward))
+    def _():
+        hop_one(0, 0).wait_send()
+
+    @pl.when(forward)
+    def _():
+        for c in range(CORES - 1):
+            hop_one(0, c).wait_recv()
+        for c in range(CORES):
+            each(lambda d: hop_one(d, c).wait_recv(), 1, hubs)
+        for j in range(group_size):
+            second[j] = arrived[table[FROM_SRC, j] & (group_size - 1)]
+        each(lambda d: hop_two(d, chip).start())
+        out_ref[pl.ds(group_size * cap + chip * relay, relay)] = second[me]
+
     base(THIRD).start()
     waiting = send(THIRD + 1, group_size - 1)
     keep = pltpu.make_async_copy(held, split_ref, own_sem.at[4])
@@ -317,8 +357,16 @@
     base(waiting).start()
     for s in range(group_size - 1):
         base(s).wait()
-    each(lambda d: hop_two(d).wait())
-    own_two.wait()
+    each(lambda d: hop_two(0, near(d)).wait_recv(), 1, hubs)
+
+    @pl.when(jnp.logical_not(forward))
+    def _():
+        hop_two(0, chip).wait_recv()
+
+    @pl.when(forward)
+    def _():
+        each(lambda d: hop_two(d, chip).wait_send())
+
     own_base.wait()
     keep.wait()
 
@@ -332,7 +380,7 @@
     return pl.pallas_call(
         functools.partial(sort_exchange_kernel, group_size, cap, relay, block),
         out_shape=[
-            pltpu.VMEM((group_size * (cap + relay), *row), rows.dtype),
+            pltpu.VMEM((group_size * cap + group_size // CORES * relay, *row), rows.dtype),
             jax.ShapeDtypeStruct(segs, keys.dtype),
             pltpu.VMEM(segs, jnp.int32),
             jax.ShapeDtypeStruct(keys.shape, jnp.int32),
@@ -348,7 +396,7 @@
             pltpu.VMEM((n // block, block, width), rows.dtype),
             pltpu.VMEM((n, *row), rows.dtype),
             pltpu.VMEM((group_size, cap, *row), rows.dtype),
-            pltpu.VMEM((group_size, relay, *row), rows.dtype),
+            pltpu.VMEM((group_size // CORES, relay, *row), rows.dtype),
             pltpu.VMEM((group_size, relay, *row), rows.dtype),
             pltpu.VMEM((group_size, relay, *row), rows.dtype),
             pltpu.VMEM(keys.shape, keys.dtype),
@@ -435,7 +483,7 @@
             staged[slot, pl.ds(r, 16), :] = jnp.stack(rows, 0).reshape(16, width)
             return c
 
-        lax.fori_loop(0, block // 16, body, 0)
+        lax.fori_loop(0, pl.cdiv(jnp.minimum(count - s * block, block), 16), body, 0)
 
         @pl.when((s + 1) * block > count)
         def _():
@@ -445,9 +493,8 @@
         store(s).start()
         return carry
 
-    lax.fori_loop(0, jnp.minimum(live, 1), step, 0)
     lax.fori_loop(live, steps, start_clear, 0)
-    lax.fori_loop(1, live, step, 0)
+    lax.fori_loop(0, live, step, 0)
 
     def end_store(s, carry):
         store(s).wait()

time: 115 us -> 114 us (level); the launches traced: 113 us -> 114 us
  no operation moved by 1% of the time
where the time goes in v9:
time: 114 us
  Pallas kernels  111 us (97%)
  between operations  2.39 us (2%)
    pallas_call x1, Pallas kernels, sort_exchange(): pl.pallas_call(functools.partial(sort_exchange_kernel, group_size, cap, r...  101 us
    pallas_call x1, Pallas kernels, place(): pl.pallas_call(place_kernel, out_shape=[jax.ShapeDtypeStruct((n_out, widt...  9.47 us

profile of v9, /device:TPU:97, one launch (start us, length us, event | category | flops | bytes accessed | tf_op | source)
XLA Modules:
  0.0 113.6 jit_solution(7805192151630503433)
XLA Ops:
  0.6 101.2 %sort_exchange.1 = (bf16[2144,3,4,128]{3,2,1,0:T(4,128)(2,1)S(1)}, f32[32,128]{1,0:T(8,128)S(1)}, s32[32,128]{1,0:T(8,128)S(1)}, s32[16,128]{1,0:T(8,128)S(1)}, ...) custom-call(f32[16,128]{1,0:T(8,128)} %bitcast.10, ...), custom_call_target="tpu_custom_call" | custom-call | tf_op jit(solution)/shard_map/sort_exchange/pallas_call | solution.py:380
  101.8 9.5 %place_rows.3 = (bf16[4096,1536]{1,0:T(8,128)(2,1)}, f32[32,128]{1,0:T(8,128)}) custom-call(s32[4096]{0:T(1024)S(1)} %bitcast.7, s32[1]{0:T(128)} %get-tuple-element.127.count_ref, bf16[2144,3,4,128]{3,2,1,0:T(4,128)(2,1)S(1)} %get-tuple-element.58.held, f32[32,128]{1,0:T(8,128)S(1)} %get-tuple-element.105.keys_ref), custom_call_target="tpu_custom_call" | custom-call | tf_op jit(solution)/shard_map/place_rows/pallas_call | solution.py:515
  111.3 0.6 while.9

commit v10 on v9

--- a/solution.py
+++ b/solution.py
@@ -447,10 +447,11 @@
     )(order, table, rows)
 
 
-def place_kernel(idx_ref, count_ref, held, keys_ref, out_ref, out_keys_ref, staged, blank, out_sem, blank_sem):
+def place_kernel(idx_ref, count_ref, held, keys_ref, out_ref, out_keys_ref, staged, blank, out_sem, blank_sem, keys_sem):
     slots, block, width = staged.shape
     parts = held.shape[1]
-    out_keys_ref[...] = keys_ref[...]
+    keys_copy = pltpu.make_async_copy(keys_ref, out_keys_ref, keys_sem)
+    keys_copy.start()
     blank[...] = jnp.zeros(blank.shape, blank.dtype)
     steps = out_ref.shape[0] // block
     count = count_ref[0]
@@ -475,15 +476,16 @@
         slot = lax.rem(s, slots)
 
         def body(g, c):
-            r = pl.multiple_of(g * 16, 16)
-            rows = []
-            for u in range(16):
-                k = idx_ref[s * block + r + u]
-                rows.append(jnp.concatenate([held[k, q] for q in range(parts)], 0))
-            staged[slot, pl.ds(r, 16), :] = jnp.stack(rows, 0).reshape(16, width)
+            for half in range(2):
+                r = pl.multiple_of(g * 32 + half * 16, 16)
+                rows = []
+                for u in range(16):
+                    k = idx_ref[s * block + r + u]
+                    rows.append(jnp.concatenate([held[k, q] for q in range(parts)], 0))
+                staged[slot, pl.ds(r, 16), :] = jnp.stack(rows, 0).reshape(16, width)
             return c
 
-        lax.fori_loop(0, pl.cdiv(jnp.minimum(count - s * block, block), 16), body, 0)
+        lax.fori_loop(0, pl.cdiv(jnp.minimum(count - s * block, block), 32), body, 0)
 
         @pl.when((s + 1) * block > count)
         def _():
@@ -507,6 +509,7 @@
         return carry
 
     lax.fori_loop(live, steps, end_clear, 0)
+    keys_copy.wait()
 
 
 def place(idx, count, rows, keys, width):
@@ -516,11 +519,12 @@
         place_kernel,
         out_shape=[jax.ShapeDtypeStruct((n_out, width), rows.dtype), jax.ShapeDtypeStruct(keys.shape, keys.dtype)],
         in_specs=[SMEM, SMEM, VMEM, VMEM],
-        out_specs=[ANY, VMEM],
+        out_specs=[ANY, ANY],
         scratch_shapes=[
             pltpu.VMEM((slots, block, width), rows.dtype),
             pltpu.VMEM((block, width), rows.dtype),
             pltpu.SemaphoreType.DMA((slots,)),
+            pltpu.SemaphoreType.DMA,
             pltpu.SemaphoreType.DMA,
         ],
         compiler_params=pltpu.CompilerParams(vmem_limit_bytes=24 * 1024 * 1024),

time: 114 us -> 113 us (level)
  Pallas kernels: 111 us -> 109 us
    pallas_call x1, Pallas kernels: 9.47 us -> 8.25 us  [place(): pl.pallas_call(place_kernel, out_shape=[jax.ShapeDtypeStruct((n_out, widt...]
where the time goes in v10:
time: 113 us; the launch traced here: 112 us
  Pallas kernels  109 us (96%)
  between operations  2.39 us (2%)
    pallas_call x1, Pallas kernels, sort_exchange(): pl.pallas_call(functools.partial(sort_exchange_kernel, group_size, cap, r...  101 us
    pallas_call x1, Pallas kernels, place(): pl.pallas_call(place_kernel, out_shape=[jax.ShapeDtypeStruct((n_out, widt...  8.25 us

profile of v10, /device:TPU:97, one launch (start us, length us, event | category | flops | bytes accessed | tf_op | source)
XLA Modules:
  0.0 112.4 jit_solution(15526886172481806303)
XLA Ops:
  0.6 101.2 %sort_exchange.1 = (bf16[2144,3,4,128]{3,2,1,0:T(4,128)(2,1)S(1)}, f32[32,128]{1,0:T(8,128)S(1)}, s32[32,128]{1,0:T(8,128)S(1)}, s32[16,128]{1,0:T(8,128)S(1)}, ...) custom-call(f32[16,128]{1,0:T(8,128)} %bitcast.10, ...), custom_call_target="tpu_custom_call" | custom-call | tf_op jit(solution)/shard_map/sort_exchange/pallas_call | solution.py:380
  101.8 8.2 %place_rows.3 = (bf16[4096,1536]{1,0:T(8,128)(2,1)}, f32[32,128]{1,0:T(8,128)}) custom-call(s32[4096]{0:T(1024)S(1)} %bitcast.7, s32[1]{0:T(128)} %get-tuple-element.127.count_ref, bf16[2144,3,4,128]{3,2,1,0:T(4,128)(2,1)S(1)} %get-tuple-element.58.held, f32[32,128]{1,0:T(8,128)S(1)} %get-tuple-element.105.keys_ref), custom_call_target="tpu_custom_call" | custom-call | tf_op jit(solution)/shard_map/place_rows/pallas_call | solution.py:518
  110.1 0.6 while.9

commit v11 on v10

--- a/solution.py
+++ b/solution.py
@@ -447,9 +447,16 @@
     )(order, table, rows)
 
 
-def place_kernel(idx_ref, count_ref, held, keys_ref, out_ref, out_keys_ref, staged, blank, out_sem, blank_sem, keys_sem):
+def place_kernel(idx_ref, count_ref, held, keys_ref, out_ref, out_keys_ref, staged, blank, idx, out_sem, blank_sem, keys_sem, idx_sem):
     slots, block, width = staged.shape
     parts = held.shape[1]
+    early = 8
+    idx_copies = [
+        pltpu.make_async_copy(idx_ref.at[pl.ds(a, b - a)], idx.at[pl.ds(a, b - a)], idx_sem.at[i])
+        for i, (a, b) in enumerate(((0, early), (early, idx_ref.shape[0])))
+    ]
+    for c in idx_copies:
+        c.start()
     keys_copy = pltpu.make_async_copy(keys_ref, out_keys_ref, keys_sem)
     keys_copy.start()
     blank[...] = jnp.zeros(blank.shape, blank.dtype)
@@ -480,7 +487,7 @@
                 r = pl.multiple_of(g * 32 + half * 16, 16)
                 rows = []
                 for u in range(16):
-                    k = idx_ref[s * block + r + u]
+                    k = idx[s, r + u]
                     rows.append(jnp.concatenate([held[k, q] for q in range(parts)], 0))
                 staged[slot, pl.ds(r, 16), :] = jnp.stack(rows, 0).reshape(16, width)
             return c
@@ -496,7 +503,10 @@
         return carry
 
     lax.fori_loop(live, steps, start_clear, 0)
-    lax.fori_loop(0, live, step, 0)
+    idx_copies[0].wait()
+    lax.fori_loop(0, jnp.minimum(live, early), step, 0)
+    idx_copies[1].wait()
+    lax.fori_loop(early, live, step, 0)
 
     def end_store(s, carry):
         store(s).wait()
@@ -513,19 +523,21 @@
 
 
 def place(idx, count, rows, keys, width):
-    n_out = idx.shape[0]
-    block, slots = 128, 4
+    n_out, block = idx.size, idx.shape[1]
+    slots = 4
     return pl.pallas_call(
         place_kernel,
         out_shape=[jax.ShapeDtypeStruct((n_out, width), rows.dtype), jax.ShapeDtypeStruct(keys.shape, keys.dtype)],
-        in_specs=[SMEM, SMEM, VMEM, VMEM],
+        in_specs=[VMEM, SMEM, VMEM, VMEM],
         out_specs=[ANY, ANY],
         scratch_shapes=[
             pltpu.VMEM((slots, block, width), rows.dtype),
             pltpu.VMEM((block, width), rows.dtype),
+            pltpu.SMEM(idx.shape, jnp.int32),
             pltpu.SemaphoreType.DMA((slots,)),
             pltpu.SemaphoreType.DMA,
             pltpu.SemaphoreType.DMA,
+            pltpu.SemaphoreType.DMA((2,)),
         ],
         compiler_params=pltpu.CompilerParams(vmem_limit_bytes=24 * 1024 * 1024),
         name="place_rows",
@@ -540,12 +552,12 @@
         width = rows_loc.shape[1]
         cap_rows = 2 * n_dev // group_size
         blocks, merged, idx, order, rows, starts, segs, own_count, short = sort_exchange(keys_loc.reshape(n_dev // LANES, LANES), rows_loc, BASE, RELAY, group_size)
-        out_rows, out_keys = place(idx.reshape(-1), own_count, blocks, merged, width)
+        out_rows, out_keys = place(idx, own_count, blocks, merged, width)
 
         def general(carry):
             wide = lax.all_to_all(pick(order.reshape(-1), starts, rows, cap_rows, group_size), "g", 0, 0, tiled=True)
             _, at = lax.sort((segs.reshape(-1), lax.iota(jnp.int32, segs.size)), num_keys=1)
-            return jnp.int32(1), place(at, own_count, wide.reshape(-1, *wide.shape[2:]), merged, width)[0]
+            return jnp.int32(1), place(at.reshape(idx.shape), own_count, wide.reshape(-1, *wide.shape[2:]), merged, width)[0]
 
         _, out_rows = lax.while_loop(lambda carry: carry[0] == 0, general, (short[0], out_rows))
         return out_keys.reshape(-1), out_rows, own_count

time: 113 us -> 114 us (level)
  no operation moved by 1% of the time
where the time goes in v11:
time: 114 us; the launch traced here: 113 us
  Pallas kernels  110 us (96%)
  between operations  2.39 us (2%)
    pallas_call x1, Pallas kernels, sort_exchange(): pl.pallas_call(functools.partial(sort_exchange_kernel, group_size, cap, r...  101 us
    pallas_call x1, Pallas kernels, place(): pl.pallas_call(place_kernel, out_shape=[jax.ShapeDtypeStruct((n_out, widt...  9.29 us

profile of v11, /device:TPU:97, one launch (start us, length us, event | category | flops | bytes accessed | tf_op | source)
XLA Modules:
  0.0 113.4 jit_solution(17744875130104034950)
XLA Ops:
  0.6 101.2 %sort_exchange.1 = (bf16[2144,3,4,128]{3,2,1,0:T(4,128)(2,1)S(1)}, f32[32,128]{1,0:T(8,128)S(1)}, s32[32,128]{1,0:T(8,128)S(1)}, s32[16,128]{1,0:T(8,128)S(1)}, ...) custom-call(f32[16,128]{1,0:T(8,128)} %bitcast.10, ...), custom_call_target="tpu_custom_call" | custom-call | tf_op jit(solution)/shard_map/sort_exchange/pallas_call | solution.py:380
  101.8 9.3 %place_rows.3 = (bf16[4096,1536]{1,0:T(8,128)(2,1)}, f32[32,128]{1,0:T(8,128)}) custom-call(s32[32,128]{1,0:T(8,128)S(1)} %get-tuple-element.56.idx_ref, s32[1]{0:T(128)} %get-tuple-element.127.count_ref, bf16[2144,3,4,128]{3,2,1,0:T(4,128)(2,1)S(1)} %get-tuple-element.58.held, f32[32,128]{1,0:T(8,128)S(1)} %get-tuple-element.105.keys_ref), custom_call_target="tpu_custom_call" | custom-call | tf_op jit(solution)/shard_map/place_rows/pallas_call | solution.py:528
  111.1 0.6 while.9

commit v12 on v10

--- a/solution.py
+++ b/solution.py
@@ -514,7 +514,7 @@
 
 def place(idx, count, rows, keys, width):
     n_out = idx.shape[0]
-    block, slots = 128, 4
+    block, slots = 128, 12
     return pl.pallas_call(
         place_kernel,
         out_shape=[jax.ShapeDtypeStruct((n_out, width), rows.dtype), jax.ShapeDtypeStruct(keys.shape, keys.dtype)],

time: 113 us -> 111 us (0.982)
    pallas_call x1, Pallas kernels: 8.25 us -> 6.84 us  [place(): pl.pallas_call(place_kernel, out_shape=[jax.ShapeDtypeStruct((n_out, widt...]
where the time goes in v12:
time: 111 us
  Pallas kernels  108 us (97%)
  between operations  2.39 us (2%)
    pallas_call x1, Pallas kernels, sort_exchange(): pl.pallas_call(functools.partial(sort_exchange_kernel, group_size, cap, r...  101 us
    pallas_call x1, Pallas kernels, place(): pl.pallas_call(place_kernel, out_shape=[jax.ShapeDtypeStruct((n_out, widt...  6.84 us

profile of v12, /device:TPU:97, one launch (start us, length us, event | category | flops | bytes accessed | tf_op | source)
XLA Modules:
  0.0 111.0 jit_solution(14684890615096781731)
XLA Ops:
  0.6 101.2 %sort_exchange.1 = (bf16[2144,3,4,128]{3,2,1,0:T(4,128)(2,1)S(1)}, f32[32,128]{1,0:T(8,128)S(1)}, s32[32,128]{1,0:T(8,128)S(1)}, s32[16,128]{1,0:T(8,128)S(1)}, ...) custom-call(f32[16,128]{1,0:T(8,128)} %bitcast.10, ...), custom_call_target="tpu_custom_call" | custom-call | tf_op jit(solution)/shard_map/sort_exchange/pallas_call | solution.py:380
  101.8 6.8 %place_rows.3 = (bf16[4096,1536]{1,0:T(8,128)(2,1)}, f32[32,128]{1,0:T(8,128)}) custom-call(s32[4096]{0:T(1024)S(1)} %bitcast.7, s32[1]{0:T(128)} %get-tuple-element.127.count_ref, bf16[2144,3,4,128]{3,2,1,0:T(4,128)(2,1)S(1)} %get-tuple-element.58.held, f32[32,128]{1,0:T(8,128)S(1)} %get-tuple-element.105.keys_ref), custom_call_target="tpu_custom_call" | custom-call | tf_op jit(solution)/shard_map/place_rows/pallas_call | solution.py:518
  108.7 0.6 while.9
